TPU v7x, 32 devices: a whole 2x2x4 slice. The times are simulated.
32 devices in a mesh: nest: 4 (over x, core), py: 2 (over y), px: 4 (over z).
Axes of the slice: x: 2, y: 2, z: 4, core: 2. Of those that a mesh axis runs over, the one named last changes fastest.
Arguments:
- initial_state: float32 [4, 4, 256, 256], P('nest', None, 'px', 'py'), may hold values from -6 to 6
- drive_modes: float32 [3, 4, 64, 64], replicated, may hold values from -6 to 6
- relax_rates: float32 [4, 4], P('nest'), may hold values from 0.2 to 0.9
- nest_offsets: int32 [4, 2], replicated, may hold values from 0 to 170
Outputs:
- final_state: float32 [4, 4, 256, 256], P('nest', None, 'px', 'py')
- final_modes: float32 [4, 4, 64, 64], P('nest')
Inputs may be any that keep to these rules, and one draw needn't show every extreme that they name: `nest_offsets`: row 0 is not read.
All inputs are finite; a program needn't handle non-finite values.
Results may differ from a plain program's by a relative error of at most 0.0001.
Values sent between devices are 32-bit elements; how exact they have to be, the bound alone decides.
A program may use at most 64 MiB of HBM per device.

v0:
```python
import math

import jax
import jax.numpy as jnp
import numpy as np
from jax import lax
from jax.sharding import PartitionSpec as P

RATIO = 3
RATE = 0.2
HI = lax.Precision.HIGH


def basis(cells, modes, refine, fn=np.cos):
    j = np.arange(modes, dtype=np.int64)
    q = 2 * np.arange(cells, dtype=np.int64) + 1
    product = (j[None, :] * q[:, None]) % (4 * refine * cells)
    weight = np.where(j == 0, 1.0, 2.0) / cells
    return np.sqrt(weight)[None, :] * fn(np.pi * product / (2.0 * refine * cells))


def half_step(table):
    pad = np.pad(table, ((1, 1), (0, 0)))
    return (0.5 - 2 * RATE) * table + RATE * (pad[2:] + pad[:-2])


def powers(table, count):
    out = [table]
    for _ in range(count):
        out.append(half_step(out[-1]))
    return out


def offset_map(cells, modes, offset):
    base = basis(cells, modes, 1)
    even = jnp.asarray(base.T @ basis(cells, modes, RATIO), jnp.float32)
    odd = jnp.asarray(base.T @ basis(cells, modes, RATIO, np.sin), jnp.float32)
    j = jnp.arange(modes, dtype=jnp.int32)
    product = (j * (2 * RATIO * offset)) % (4 * RATIO * cells)
    angle = jnp.pi * product.astype(jnp.float32) / (2.0 * RATIO * cells)
    return even * jnp.cos(angle)[None, :] - odd * jnp.sin(angle)[None, :]


def exchange(value, axis, dim, width):
    n, length = lax.axis_size(axis), value.shape[dim]
    up = [(i, i + 1) for i in range(n - 1)]
    down = [(i + 1, i) for i in range(n - 1)]
    before = lax.ppermute(lax.slice_in_dim(value, length - width, length, axis=dim), axis, up)
    after = lax.ppermute(lax.slice_in_dim(value, 0, width, axis=dim), axis, down)
    return jnp.concatenate([before, value, after], axis=dim)


def free_steps(field, total_x, total_y, steps):
    levels, cx, cy = field.shape
    pad = exchange(exchange(field, "py", 2, steps), "px", 1, steps)
    gx = lax.axis_index("px") * cx - steps + jnp.arange(cx + 2 * steps)
    gy = lax.axis_index("py") * cy - steps + jnp.arange(cy + 2 * steps)
    inside = ((gx >= 0) & (gx < total_x))[:, None] & ((gy >= 0) & (gy < total_y))[None, :]
    for s in range(steps):
        mid = pad[:, 1:-1, 1:-1]
        near = pad[:, 2:, 1:-1] + pad[:, :-2, 1:-1] + pad[:, 1:-1, 2:] + pad[:, 1:-1, :-2]
        pad = mid + RATE * (near - 4.0 * mid)
        cut = s + 1
        pad = jnp.where(inside[cut:-cut, cut:-cut][None], pad, 0.0)
    return pad


def body(initial_state, drive_modes, relax_rates, nest_offsets):
    k = lax.axis_index("nest")
    nests = lax.axis_size("nest")
    field = initial_state[0]
    levels, cx, cy = field.shape
    windows, _, m, _ = drive_modes.shape
    nx, ny = cx * lax.axis_size("px"), cy * lax.axis_size("py")
    rp, cp = powers(basis(nx, m, 1), windows), powers(basis(ny, m, 1), windows)
    a = [jnp.asarray(rp[0].T @ t, jnp.float32) for t in rp]
    b = [jnp.asarray(cp[0].T @ t, jnp.float32) for t in cp]
    u_all = jnp.asarray(np.concatenate(rp, 1), jnp.float32)
    v_all = jnp.asarray(np.concatenate(cp, 1), jnp.float32)
    u = lax.dynamic_slice_in_dim(u_all, lax.axis_index("px") * cx, cx, 0)
    v = lax.dynamic_slice_in_dim(v_all, lax.axis_index("py") * cy, cy, 0)

    half = jnp.einsum("lxy,yq->lxq", field, v, precision=HI)
    rows = []
    for w in range(1, windows + 1):
        terms = [math.comb(w, i) * half[:, :, (w - i) * m : (w - i + 1) * m] for i in range(w + 1)]
        rows.append(
            jnp.einsum(
                "xj,lxm->ljm",
                jnp.concatenate([u[:, i * m : (i + 1) * m] for i in range(w + 1)], 0),
                jnp.concatenate(terms, 1),
                precision=HI,
            )
        )
    shares = lax.psum(jnp.stack(rows), ("py", "px"))

    gain = relax_rates[0][:, None, None]
    row_map = offset_map(nx, m, nest_offsets[k, 0])
    col_map = offset_map(ny, m, nest_offsets[k, 1])

    def left(t, x):
        return jnp.einsum("jp,lpq->ljq", t, x, precision=HI)

    def right(x, t):
        return jnp.einsum("ljq,mq->ljm", x, t, precision=HI)

    def spread(d, x):
        out = left(a[d], x) + right(x, b[d])
        for i in range(1, d):
            out = out + math.comb(d, i) * right(left(a[i], x), b[d - i])
        return out

    parent = jnp.zeros_like(drive_modes)
    for stage in range(nests):
        if stage:
            parent = lax.ppermute(coeffs, "nest", [(i, i + 1) for i in range(nests - 1)])
            interp = jnp.einsum("jp,wlpq->wljq", row_map, parent, precision=HI)
            interp = jnp.einsum("wljq,mq->wljm", interp, col_map, precision=HI)
            target = jnp.where(k == 0, drive_modes, interp)
        else:
            target = drive_modes
        changes, kept = [], []
        for w in range(windows):
            own = shares[w]
            for e in range(w):
                own = own + spread(w - e, changes[e])
            changes.append(gain * (target[w] - own))
            kept.append(own + changes[-1])
        coeffs = jnp.stack(kept)

    free = free_steps(field, nx, ny, windows)
    zero = jnp.zeros_like(changes[0])
    blocks = [
        jnp.concatenate(
            [
                math.comb(i + j, i) * changes[windows - 1 - i - j] if i + j < windows else zero
                for j in range(windows)
            ],
            2,
        )
        for i in range(windows)
    ]
    mixed = jnp.concatenate(blocks, 1)
    wide = windows * m
    back = jnp.einsum("lpq,yq->lpy", mixed, v[:, :wide], precision=HI)
    final = free + jnp.einsum("xp,lpy->lxy", u[:, :wide], back, precision=HI)
    return final[None], coeffs[windows - 1][None]


def solution(mesh):
    spec = P("nest", None, "px", "py")
    return jax.shard_map(
        body,
        mesh=mesh,
        in_specs=(spec, P(), P("nest", None), P()),
        out_specs=(spec, P("nest", None, None, None)),
        check_vma=False,
    )
```

profile of v0, /device:TPU:1, one launch (start us, length us, event | category | flops | bytes accessed | tf_op | source)
XLA Modules:
  0.0 132.8 jit_solution(5296330586854888723)
XLA Ops:
  7.2 1.2 convolution_bitcast_fusion.3
  8.6 0.8 copy-done.7
  10.4 0.8 pad_maximum_fusion
  11.2 0.9 copy-done.3
  12.2 4.1 %collective-permute-start = (f32[4,64,3]{2,1,0:T(8,128)S(1)}, f32[4,64,3]{2,1,0:T(8,128)S(1)}, u32[]{:S(2)}, u32[]{:S(2)}) collective-permute-start(f32[4,64,3]{2,1,0:T(8,128)S(1)} %get-tuple-element.23), channel_id=1, source_target_pairs={{0,4},{1,5},{2,6},{3,7},{8,12},{9,13},{10,14},{11,15},{16,20},{17,... | collective-permute-start | bytes 9224 | tf_op jit(solution)/shard_map/ppermute | solution.py:48
  16.3 1.3 collective-permute-start.1
  17.6 0.7 copy-done.9
  18.3 0.6 constant_dynamic-slice_fusion.2
  20.3 4.1 %collective-permute-done.1 = f32[4,64,3]{2,1,0:T(8,128)S(1)} collective-permute-done((f32[4,64,3]{2,1,0:T(8,128)S(1)}, f32[4,64,3]{2,1,0:T(8,128)S(1)}, u32[]{:S(2)}, u32[]{:S(2)}) %collective-permute-start.1) | collective-permute-done | bytes 3104 | tf_op jit(solution)/shard_map/ppermute | solution.py:49
  24.6 3.2 %collective-permute-start.2 = (f32[4,3,134]{2,1,0:T(4,128)S(1)}, f32[4,3,134]{2,1,0:T(4,128)S(1)}, u32[]{:S(2)}, u32[]{:S(2)}) collective-permute-start(f32[4,3,134]{2,1,0:T(4,128)S(1)} %get-tuple-element.10), channel_id=1, source_target_pairs={{0,1},{1,2},{2,3},{4,5},{5,6},{6,7},{8,9},{9,10},{10,11},{12,13},{... | collective-permute-start | bytes 19304 | tf_op jit(solution)/shard_map/ppermute | solution.py:48
  27.8 1.3 collective-permute-start.3
  29.1 54.7 %all-reduce.3.cloned.1.call-done = f32[3,4,64,64]{3,2,1,0:T(8,128)} async-done(((f32[3,4,64,64]{3,2,1,0:T(8,128)}), f32[3,4,64,64]{3,2,1,0:T(8,128)}) %all-reduce.3.cloned.1.call-update) | async-done | bytes 196624 | tf_op jit(solution)/shard_map/psum | solution.py:95
  83.8 1.0 bitcast_multiply_fusion.2
  85.2 0.6 copy-done.2
  86.7 0.5 copy-done.4
  87.7 5.6 %collective-permute-start.4 = (f32[3,4,64,64]{3,2,1,0:T(8,128)S(1)}, f32[3,4,64,64]{3,2,1,0:T(8,128)S(1)}, u32[]{:S(2)}, u32[]{:S(2)}) collective-permute-start(f32[3,4,64,64]{3,2,1,0:T(8,128)S(1)} %pad_maximum_fusion.1), channel_id=1, source_target_pairs={{0,8},{8,16},{16,24},{1,9},{9,17},{17,25},{2,10},{10,18},{18,26},{... | collective-permute-start | bytes 589832 | tf_op jit(solution)/shard_map/ppermute | solution.py:116
  94.0 4.1 %collective-permute-done.4 = f32[3,4,64,64]{3,2,1,0:T(8,128)S(1)} collective-permute-done((f32[3,4,64,64]{3,2,1,0:T(8,128)S(1)}, f32[3,4,64,64]{3,2,1,0:T(8,128)S(1)}, u32[]{:S(2)}, u32[]{:S(2)}) %collective-permute-start.4) | collective-permute-done | bytes 196640 | tf_op jit(solution)/shard_map/ppermute | solution.py:116
  100.7 4.4 %collective-permute-start.5 = (f32[3,4,64,64]{3,2,1,0:T(8,128)S(1)}, f32[3,4,64,64]{3,2,1,0:T(8,128)S(1)}, u32[]{:S(2)}, u32[]{:S(2)}) collective-permute-start(f32[3,4,64,64]{3,2,1,0:T(8,128)S(1)} %pad_maximum_fusion.2), channel_id=1, source_target_pairs={{0,8},{8,16},{16,24},{1,9},{9,17},{17,25},{2,10},{10,18},{18,26},{... | collective-permute-start | bytes 589832 | tf_op jit(solution)/shard_map/ppermute | solution.py:116
  105.5 4.3 %collective-permute-done.5 = f32[3,4,64,64]{3,2,1,0:T(8,128)S(1)} collective-permute-done((f32[3,4,64,64]{3,2,1,0:T(8,128)S(1)}, f32[3,4,64,64]{3,2,1,0:T(8,128)S(1)}, u32[]{:S(2)}, u32[]{:S(2)}) %collective-permute-start.5) | collective-permute-done | bytes 196640 | tf_op jit(solution)/shard_map/ppermute | solution.py:116
  112.6 4.4 %collective-permute-start.6 = (f32[3,4,64,64]{3,2,1,0:T(8,128)S(1)}, f32[3,4,64,64]{3,2,1,0:T(8,128)S(1)}, u32[]{:S(2)}, u32[]{:S(2)}) collective-permute-start(f32[3,4,64,64]{3,2,1,0:T(8,128)S(1)} %pad_maximum_fusion.3), channel_id=1, source_target_pairs={{0,8},{8,16},{16,24},{1,9},{9,17},{17,25},{2,10},{10,18},{18,26},{... | collective-permute-start | bytes 589832 | tf_op jit(solution)/shard_map/ppermute | solution.py:116
  117.3 4.3 %collective-permute-done.6 = f32[3,4,64,64]{3,2,1,0:T(8,128)S(1)} collective-permute-done((f32[3,4,64,64]{3,2,1,0:T(8,128)S(1)}, f32[3,4,64,64]{3,2,1,0:T(8,128)S(1)}, u32[]{:S(2)}, u32[]{:S(2)}) %collective-permute-start.6) | collective-permute-done | bytes 196640 | tf_op jit(solution)/shard_map/ppermute | solution.py:116
  123.6 0.9 add_bitcast_fusion
  124.5 0.5 fusion.20
  125.1 0.9 fusion.1
  (83 shorter events, 11.7 us)
Async XLA Ops:
  7.2 76.6 %all-reduce.3.cloned.1.call-start = ((), (), s32[]{:S(2)}) async-start(), calls=%async_computation | async-start | bytes 786432 | tf_op jit(solution)/shard_map/psum | solution.py:95
  8.4 1.0 copy-start.7
  11.2 0.9 copy-start.3
  12.1 71.7 %copy-start.1 = (f32[3,4,64,64]{3,2,1,0:T(8,128)S(1)}, f32[3,4,64,64]{3,2,1,0:T(8,128)}, u32[]{:S(2)}) copy-start(f32[3,4,64,64]{3,2,1,0:T(8,128)} %param.15) | copy-start | bytes 589828
  12.2 8.2 %collective-permute-start = (f32[4,64,3]{2,1,0:T(8,128)S(1)}, f32[4,64,3]{2,1,0:T(8,128)S(1)}, u32[]{:S(2)}, u32[]{:S(2)}) collective-permute-start(f32[4,64,3]{2,1,0:T(8,128)S(1)} %get-tuple-element.23), channel_id=1, source_target_pairs={{0,4},{1,5},{2,6},{3,7},{8,12},{9,13},{10,14},{11,15},{16,20},{17,... | collective-permute-start | bytes 9224 | tf_op jit(solution)/shard_map/ppermute | solution.py:48
  16.3 8.2 %collective-permute-start.1 = (f32[4,64,3]{2,1,0:T(8,128)S(1)}, f32[4,64,3]{2,1,0:T(8,128)S(1)}, u32[]{:S(2)}, u32[]{:S(2)}) collective-permute-start(f32[4,64,3]{2,1,0:T(8,128)S(1)} %get-tuple-element.24), channel_id=1, source_target_pairs={{4,0},{5,1},{6,2},{7,3},{12,8},{13,9},{14,10},{15,11},{20,16},{21,... | collective-permute-start | bytes 9224 | tf_op jit(solution)/shard_map/ppermute | solution.py:49
  17.6 0.7 copy-start.9
  24.6 69.2 %collective-permute-start.2 = (f32[4,3,134]{2,1,0:T(4,128)S(1)}, f32[4,3,134]{2,1,0:T(4,128)S(1)}, u32[]{:S(2)}, u32[]{:S(2)}) collective-permute-start(f32[4,3,134]{2,1,0:T(4,128)S(1)} %get-tuple-element.10), channel_id=1, source_target_pairs={{0,1},{1,2},{2,3},{4,5},{5,6},{6,7},{8,9},{9,10},{10,11},{12,13},{... | collective-permute-start | bytes 19304 | tf_op jit(solution)/shard_map/ppermute | solution.py:48
  27.8 56.0 %copy-start.8 = (f32[1,4]{1,0:T(1,128)S(1)}, f32[1,4]{1,0:T(1,128)}, u32[]{:S(2)}) copy-start(f32[1,4]{1,0:T(1,128)} %param.16) | copy-start | bytes 52
  27.8 65.9 %collective-permute-start.3 = (f32[4,3,134]{2,1,0:T(4,128)S(1)}, f32[4,3,134]{2,1,0:T(4,128)S(1)}, u32[]{:S(2)}, u32[]{:S(2)}) collective-permute-start(f32[4,3,134]{2,1,0:T(4,128)S(1)} %get-tuple-element.11), channel_id=1, source_target_pairs={{1,0},{2,1},{3,2},{5,4},{6,5},{7,6},{9,8},{10,9},{11,10},{13,12},{... | collective-permute-start | bytes 19304 | tf_op jit(solution)/shard_map/ppermute | solution.py:49
  83.8 1.0 copy-start
  84.8 1.0 copy-start.2
  86.4 0.8 copy-start.4
  87.7 10.3 %collective-permute-start.4 = (f32[3,4,64,64]{3,2,1,0:T(8,128)S(1)}, f32[3,4,64,64]{3,2,1,0:T(8,128)S(1)}, u32[]{:S(2)}, u32[]{:S(2)}) collective-permute-start(f32[3,4,64,64]{3,2,1,0:T(8,128)S(1)} %pad_maximum_fusion.1), channel_id=1, source_target_pairs={{0,8},{8,16},{16,24},{1,9},{9,17},{17,25},{2,10},{10,18},{18,26},{... | collective-permute-start | bytes 589832 | tf_op jit(solution)/shard_map/ppermute | solution.py:116
  93.7 4.3 %copy-start.5 = (f32[64,64]{1,0:T(8,128)S(1)}, f32[64,64]{1,0:T(8,128)}, u32[]{:S(2)}) copy-start(f32[64,64]{1,0:T(8,128)} %constant.86.clone) | copy-start | bytes 49156
  93.7 4.3 %copy-start.6 = (f32[64,64]{1,0:T(8,128)S(1)}, f32[64,64]{1,0:T(8,128)}, u32[]{:S(2)}) copy-start(f32[64,64]{1,0:T(8,128)} %constant.87.clone) | copy-start | bytes 49156
  100.7 9.1 %collective-permute-start.5 = (f32[3,4,64,64]{3,2,1,0:T(8,128)S(1)}, f32[3,4,64,64]{3,2,1,0:T(8,128)S(1)}, u32[]{:S(2)}, u32[]{:S(2)}) collective-permute-start(f32[3,4,64,64]{3,2,1,0:T(8,128)S(1)} %pad_maximum_fusion.2), channel_id=1, source_target_pairs={{0,8},{8,16},{16,24},{1,9},{9,17},{17,25},{2,10},{10,18},{18,26},{... | collective-permute-start | bytes 589832 | tf_op jit(solution)/shard_map/ppermute | solution.py:116
  112.6 9.1 %collective-permute-start.6 = (f32[3,4,64,64]{3,2,1,0:T(8,128)S(1)}, f32[3,4,64,64]{3,2,1,0:T(8,128)S(1)}, u32[]{:S(2)}, u32[]{:S(2)}) collective-permute-start(f32[3,4,64,64]{3,2,1,0:T(8,128)S(1)} %pad_maximum_fusion.3), channel_id=1, source_target_pairs={{0,8},{8,16},{16,24},{1,9},{9,17},{17,25},{2,10},{10,18},{18,26},{... | collective-permute-start | bytes 589832 | tf_op jit(solution)/shard_map/ppermute | solution.py:116
Sparse Core Ops, SparseCore 0:
  11.3 72.4 all-reduce.2
where the time goes:
time: 133 us
  waiting for transfers between devices  71.5 us (54%)
  starting transfers between devices  24.4 us (18%)
  between operations  16 us (12%)
  matrix products  12.6 us (9%)
  local copies, waits for them, and re-layouts  4.49 us (3%)
  other arithmetic  3.84 us (3%)
    psum x1, waiting for transfers between devices, body(): shares = lax.psum(jnp.stack(rows), ('py', 'px'))  54.7 us
    ppermute x3, starting transfers between devices, body(): lax.ppermute(coeffs, 'nest', [(i, i + 1) for i in range(nests - 1)])  14.4 us
    ppermute x3, waiting for transfers between devices, body(): lax.ppermute(coeffs, 'nest', [(i, i + 1) for i in range(nests - 1)])  12.7 us
    ppermute x2, starting transfers between devices, exchange(): lax.ppermute(lax.slice_in_dim(value, length - width, length, axis=dim), a...  7.35 us
    dot_general x16, matrix products, right(): return jnp.einsum('ljq,mq->ljm', x, t, precision=HI)  4.38 us
    ppermute x2, waiting for transfers between devices, exchange(): lax.ppermute(lax.slice_in_dim(value, 0, width, axis=dim), axis, down)  4.13 us
    unnamed x20, local copies, waits for them, and re-layouts  3.45 us
    dot_general x12, matrix products, left(): return jnp.einsum('jp,lpq->ljq', t, x, precision=HI)  2.86 us
  transfers between devices with their start and end apart: 8, of which 5 were waited for; matrix products, arithmetic and copies ran while one was open for 4% of the time, Pallas kernels for 0%

commit v1 on v0

v1 whole, which is shorter than its diff:
```python
import functools
import math

import jax
import jax.numpy as jnp
import numpy as np
from jax import lax
from jax.experimental import pallas as pl
from jax.experimental.pallas import tpu as pltpu
from jax.sharding import PartitionSpec as P

RATIO = 3
RATE = 0.2
MESH = pl.DeviceIdType.MESH
F32, BF16 = jnp.float32, jnp.bfloat16


def basis(cells, modes, refine, fn=np.cos):
    j = np.arange(modes, dtype=np.int64)
    q = 2 * np.arange(cells, dtype=np.int64) + 1
    product = (j[None, :] * q[:, None]) % (4 * refine * cells)
    weight = np.where(j == 0, 1.0, 2.0) / cells
    return np.sqrt(weight)[None, :] * fn(np.pi * product / (2.0 * refine * cells))


def half_step(table):
    pad = np.pad(table, ((1, 1), (0, 0)))
    return (0.5 - 2 * RATE) * table + RATE * (pad[2:] + pad[:-2])


def powers(table, count):
    out = [table]
    for _ in range(count):
        out.append(half_step(out[-1]))
    return out


def halves(table):
    high = np.asarray(table, np.float32).astype(BF16)
    low = (np.asarray(table, np.float64) - high.astype(np.float64)).astype(np.float32)
    return np.stack([high, low.astype(BF16)])


def split(x):
    high = x.astype(BF16)
    return high, (x - high.astype(F32)).astype(BF16)


def mm(a, b):
    return lax.dot_general(a, b, (((1,), (0,)), ((), ())), preferred_element_type=F32)


def dot3(a, b):
    a = a if isinstance(a, tuple) else split(a)
    b = b if isinstance(b, tuple) else split(b)
    return mm(a[0], b[0]) + (mm(a[0], b[1]) + mm(a[1], b[0]))


def loop(n, fn):
    if n <= 16:
        for i in range(n):
            fn(i)
    else:
        lax.fori_loop(0, n, lambda i, c: (fn(i), c)[1], 0)


def kernel(
    dims, owners,
    field, drive, relax, offs, u_hbm, ut_hbm, v_hbm, vt_hbm, small_hbm,
    out, modes,
    fvm, fbuf, gbuf, fin, par, cbuf, tx, u_t, ut_t, v_t, vt_t, small,
    load_sem, a_send, a_recv, c_send, c_recv, f_send, f_recv, m_send, m_recv,
):
    nests, PY, PX, L, cx, cy, m, W = dims
    G, nx, ny = PY * PX, cx * PX, cy * PY
    k, py, px = lax.axis_index("nest"), lax.axis_index("py"), lax.axis_index("px")
    me = px * PY + py
    mine = [me == o for o in owners]
    level = sum(jnp.where(c, l, 0) for l, c in enumerate(mine))
    is_owner = functools.reduce(jnp.logical_or, mine)

    def at(g):
        return (k, g % PY, g // PY)

    def plain(g):
        return functools.reduce(jnp.logical_and, [g != o for o in owners])

    barrier = pltpu.get_barrier_semaphore()
    for l, o in enumerate(owners):
        @pl.when(me != o)
        def _():
            pl.semaphore_signal(barrier, inc=1, device_id=at(o), device_id_type=MESH)

    @pl.when(is_owner)
    def _():
        def greet(g):
            @pl.when(plain(g))
            def _():
                pl.semaphore_signal(barrier, inc=1, device_id=at(g), device_id_type=MESH)
        loop(G, greet)

        @pl.when(k > 0)
        def _():
            pl.semaphore_signal(barrier, inc=1, device_id=(k - 1, py, px), device_id_type=MESH)

        @pl.when(k < nests - 1)
        def _():
            pl.semaphore_signal(barrier, inc=1, device_id=(k + 1, py, px), device_id_type=MESH)

    loads = [pltpu.make_async_copy(field.at[0, l], fvm.at[l], load_sem.at[l]) for l in range(L)]
    for c in loads:
        c.start()
    tables = [
        pltpu.make_async_copy(src, dst, load_sem.at[L + i])
        for i, (src, dst) in enumerate(
            [(v_hbm, v_t), (ut_hbm, ut_t), (small_hbm, small), (u_hbm, u_t), (vt_hbm, vt_t)]
        )
    ]
    get_drive = pltpu.make_async_copy(drive.at[:, level], par, load_sem.at[L + 5])

    @pl.when(is_owner)
    def _():
        for c in tables:
            c.start()

        @pl.when(k == 0)
        def _():
            get_drive.start()

        pl.semaphore_wait(
            barrier, G - 1 + jnp.where(k > 0, 1, 0) + jnp.where(k < nests - 1, 1, 0)
        )

    @pl.when(jnp.logical_not(is_owner))
    def _():
        pl.semaphore_wait(barrier, L)

    def patch(ref, g, shift):
        return ref.at[
            pl.ds(pl.multiple_of((g // PY) * cx + shift, 8), cx),
            pl.ds(pl.multiple_of((g % PY) * cy, 128), cy),
        ]

    def gather(l):
        return pltpu.make_async_remote_copy(
            src_ref=fvm.at[l], dst_ref=patch(fbuf, me, 8), send_sem=a_send.at[l],
            recv_sem=a_recv.at[me], device_id=at(owners[l]), device_id_type=MESH,
        )

    def keep(l):
        return pltpu.make_async_copy(fvm.at[l], patch(fbuf, me, 8), a_send.at[l])

    for l, o in enumerate(owners):
        loads[l].wait()

        @pl.when(me != o)
        def _():
            gather(l).start()

        @pl.when(me == o)
        def _():
            keep(l).start()

    @pl.when(is_owner)
    def _():
        edge = jnp.zeros((8, ny), F32)
        for ref in (fbuf, gbuf):
            ref[0:8, :] = edge
            ref[nx + 8 : nx + 16, :] = edge
        tables[2].wait()
        gain = relax[0, level]
        rest = 2.0 * (1.0 - gain)

        def turn(cells, dim, axis):
            number = lax.broadcasted_iota(jnp.int32, (m, m), dim).astype(F32)
            product = number * (2 * RATIO * offs[k, axis]).astype(F32)
            period = float(4 * RATIO * cells)
            product = product - period * jnp.floor(product * (1.0 / period))
            angle = product * (math.pi / (2.0 * RATIO * cells))
            return jnp.cos(angle), jnp.sin(angle)

        eye = jnp.where(
            lax.broadcasted_iota(jnp.int32, (m, m), 0) == lax.broadcasted_iota(jnp.int32, (m, m), 1),
            1.0, 0.0,
        ).astype(F32)
        cos_x, sin_x = turn(nx, 1, 0)
        cos_y, sin_y = turn(ny, 0, 1)
        row = jnp.where(k == 0, eye, small[0] * cos_x - small[1] * sin_x)
        col = jnp.where(k == 0, eye, small[2] * cos_y - small[3] * sin_y)
        a1, b1 = split(small[4]), split(small[7])
        a2 = split(small[5] - gain * small[6])
        b2 = split(small[8] - gain * small[9])
        f0, g0 = split(row), split(col)
        f1, f2 = split(dot3(a1, f0)), split(dot3(a2, f0))
        g1, g2 = split(dot3(g0, b1)), split(dot3(g0, b2))

        def follow():
            c1, c2, c3 = (split(par[w]) for w in range(W))
            y10, y20, y30 = dot3(c1, g0), dot3(c2, g0), dot3(c3, g0)
            y11, y21, y12 = dot3(c1, g1), dot3(c2, g1), dot3(c1, g2)
            y10s = split(y10)
            tx[0] = dot3(f0, y10s)
            tx[1] = dot3(f0, y20)
            tx[2] = dot3(f0, y30)
            tx[3] = dot3(f1, y10s) + dot3(f0, y11)
            tx[4] = dot3(f0, y21 + y12) + dot3(f1, y20 + rest * y11) + dot3(f2, y10s)

        @pl.when(k == 0)
        def _():
            get_drive.wait()
            follow()

        tables[0].wait()
        tables[1].wait()

        def arrive(g):
            @pl.when(g == me)
            def _():
                keep(level).wait()

            @pl.when(g != me)
            def _():
                pltpu.make_async_remote_copy(
                    src_ref=fvm.at[0], dst_ref=patch(fbuf, g, 8), send_sem=a_send.at[0],
                    recv_sem=a_recv.at[g], device_id=at(me), device_id_type=MESH,
                ).wait_recv()
        loop(G, arrive)

        step = min(nx, 256)
        both = jnp.zeros(((W + 1) * m, (W + 1) * m), F32)
        for r in range(0, nx, step):
            part = dot3(fbuf[8 + r : 8 + r + step, :], (v_t[0], v_t[1]))
            both = both + dot3((ut_t[0, :, r : r + step], ut_t[1, :, r : r + step]), part)

        def block(i, j):
            return both[i * m : (i + 1) * m, j * m : (j + 1) * m]

        s1, s2, s3 = (
            sum(float(math.comb(w, i)) * block(i, w - i) for i in range(w + 1)) for w in (1, 2, 3)
        )
        s1s, s2s = split(s1), split(s2)
        z11 = dot3(s1s, b1)
        x2 = dot3(a1, s1s) + z11
        x3 = dot3(s2s, b1) + dot3(s1s, b2) + dot3(a1, s2 + rest * z11) + dot3(a2, s1s)
        o2, o3 = s2 - gain * x2, s3 - gain * x3

        rows = 32

        def free():
            col_id = lax.broadcasted_iota(jnp.int32, (rows, ny), 1)

            def sweep(src, dst):
                def some(r, carry):
                    start = pl.multiple_of(r * rows, 8)
                    wide = src[pl.ds(start, rows + 16), :]
                    mid = wide[8 : rows + 8]
                    near = wide[7 : rows + 7] + wide[9 : rows + 9]
                    near = near + jnp.where(col_id == 0, 0.0, pltpu.roll(mid, 1, 1))
                    near = near + jnp.where(col_id == ny - 1, 0.0, pltpu.roll(mid, ny - 1, 1))
                    dst[pl.ds(pl.multiple_of(start + 8, 8), rows), :] = mid + RATE * (near - 4.0 * mid)
                    return carry
                lax.fori_loop(0, nx // rows, some, 0)
            sweep(fbuf, gbuf)
            sweep(gbuf, fbuf)
            sweep(fbuf, gbuf)

        chain_in = pltpu.make_async_remote_copy(
            src_ref=cbuf, dst_ref=par, send_sem=c_send, recv_sem=c_recv,
            device_id=(k, py, px), device_id_type=MESH,
        )
        chain_out = pltpu.make_async_remote_copy(
            src_ref=cbuf, dst_ref=par, send_sem=c_send, recv_sem=c_recv,
            device_id=(k + 1, py, px), device_id_type=MESH,
        )

        @pl.when(k > 0)
        def _():
            free()
            chain_in.wait_recv()
            follow()

        own2, own3 = o2 + gain * tx[3], o3 + gain * tx[4]
        d1, d2, d3 = gain * (tx[0] - s1), gain * (tx[1] - own2), gain * (tx[2] - own3)
        cbuf[0] = s1 + d1
        cbuf[1] = own2 + d2
        cbuf[2] = own3 + d3

        @pl.when(k < nests - 1)
        def _():
            chain_out.start()

        def tell(g):
            return pltpu.make_async_remote_copy(
                src_ref=cbuf.at[W - 1], dst_ref=modes.at[0, level], send_sem=m_send.at[g],
                recv_sem=m_recv.at[level], device_id=at(g), device_id_type=MESH,
            )

        def tell_start(g):
            @pl.when(g != me)
            def _():
                tell(g).start()
        loop(G, tell_start)
        own_modes = pltpu.make_async_copy(cbuf.at[W - 1], modes.at[0, level], m_recv.at[level])
        own_modes.start()

        @pl.when(k == 0)
        def _():
            free()

        tables[3].wait()
        tables[4].wait()
        e1, e2, e3 = split(d1), split(d2), split(d3)
        vt = [(vt_t[0, i * m : (i + 1) * m, :], vt_t[1, i * m : (i + 1) * m, :]) for i in range(W)]
        w0 = dot3(e3, vt[0]) + dot3(e2, vt[1]) + dot3(e1, vt[2])
        w1 = dot3(e2, vt[0]) + 2.0 * dot3(e1, vt[1])
        w2 = dot3(e1, vt[0])
        mixed = split(jnp.concatenate([w0, w1, w2], 0))

        def send_back(g):
            return pltpu.make_async_remote_copy(
                src_ref=patch(fin, g, 0), dst_ref=out.at[0, level], send_sem=f_send.at[g],
                recv_sem=f_recv.at[level], device_id=at(g), device_id_type=MESH,
            )

        own_out = pltpu.make_async_copy(patch(fin, me, 0), out.at[0, level], f_recv.at[level])

        def finish(r):
            here = pl.ds(pl.multiple_of(r * cx, 8), cx)
            there = pl.ds(pl.multiple_of(r * cx + 8, 8), cx)
            fin[here, :] = gbuf[there, :] + dot3((u_t[0, here, :], u_t[1, here, :]), mixed)

            def give(j):
                g = r * PY + j

                @pl.when(g != me)
                def _():
                    send_back(g).start()

                @pl.when(g == me)
                def _():
                    own_out.start()
            loop(PY, give)
        loop(PX, finish)

        own_out.wait()
        own_modes.wait()

        def drain(g):
            @pl.when(g != me)
            def _():
                tell(g).wait_send()
                send_back(g).wait_send()
        loop(G, drain)

        @pl.when(k < nests - 1)
        def _():
            chain_out.wait_send()

    for l, o in enumerate(owners):
        @pl.when(me != o)
        def _():
            pltpu.make_async_remote_copy(
                src_ref=cbuf.at[W - 1], dst_ref=modes.at[0, l], send_sem=m_send.at[0],
                recv_sem=m_recv.at[l], device_id=at(o), device_id_type=MESH,
            ).wait_recv()
            pltpu.make_async_remote_copy(
                src_ref=patch(fin, 0, 0), dst_ref=out.at[0, l], send_sem=f_send.at[0],
                recv_sem=f_recv.at[l], device_id=at(o), device_id_type=MESH,
            ).wait_recv()
            gather(l).wait_send()


def body(dims, owners, initial_state, drive_modes, relax_rates, nest_offsets):
    nests, PY, PX, L, cx, cy, m, W = dims
    G, nx, ny = PY * PX, cx * PX, cy * PY
    rp, cp = powers(basis(nx, m, 1), W), powers(basis(ny, m, 1), W)
    u, v = np.concatenate(rp, 1), np.concatenate(cp, 1)
    a = [rp[0].T @ t for t in rp]
    b = [cp[0].T @ t for t in cp]
    even_x, odd_x = (rp[0].T @ basis(nx, m, RATIO, f) for f in (np.cos, np.sin))
    even_y, odd_y = ((cp[0].T @ basis(ny, m, RATIO, f)).T for f in (np.cos, np.sin))
    small = np.stack(
        [even_x, odd_x, even_y, odd_y, a[1], a[2], a[1] @ a[1], b[1], b[2], b[1] @ b[1]]
    ).astype(np.float32)
    wide, deep = W * m, (W + 1) * m
    tables = (halves(u[:, :wide]), halves(u.T), halves(v), halves(v.T[:wide]))
    any_space = pl.BlockSpec(memory_space=pl.ANY)
    vmem = pl.BlockSpec(memory_space=pltpu.VMEM)
    smem = pl.BlockSpec(memory_space=pltpu.SMEM)
    dma = pltpu.SemaphoreType.DMA
    return pl.pallas_call(
        functools.partial(kernel, dims, owners),
        out_shape=(
            jax.ShapeDtypeStruct((1, L, cx, cy), F32),
            jax.ShapeDtypeStruct((1, L, m, m), F32),
        ),
        in_specs=[any_space, any_space, smem, smem] + [any_space] * 5,
        out_specs=(vmem, vmem),
        scratch_shapes=[
            pltpu.VMEM((L, cx, cy), F32),
            pltpu.VMEM((nx + 16, ny), F32),
            pltpu.VMEM((nx + 16, ny), F32),
            pltpu.VMEM((nx, ny), F32),
            pltpu.VMEM((W, m, m), F32),
            pltpu.VMEM((W, m, m), F32),
            pltpu.VMEM((5, m, m), F32),
            pltpu.VMEM((2, nx, wide), BF16),
            pltpu.VMEM((2, deep, nx), BF16),
            pltpu.VMEM((2, ny, deep), BF16),
            pltpu.VMEM((2, wide, ny), BF16),
            pltpu.VMEM((10, m, m), F32),
            dma((L + 6,)),
            dma((L,)),
            dma((G,)),
            dma,
            dma,
            dma((G,)),
            dma((L,)),
            dma((G,)),
            dma((L,)),
        ],
        compiler_params=pltpu.CompilerParams(collective_id=0, has_side_effects=True),
    )(initial_state, drive_modes, relax_rates, nest_offsets,
      *(jnp.asarray(t) for t in tables), jnp.asarray(small))


def solution(mesh):
    nests, PY, PX = (mesh.shape[n] for n in ("nest", "py", "px"))
    spec = P("nest", None, "px", "py")

    def local(initial_state, drive_modes, relax_rates, nest_offsets):
        _, L, cx, cy = initial_state.shape
        W, _, m, _ = drive_modes.shape
        places = sorted(
            range(PY * PX),
            key=lambda g: (abs(2 * (g // PY) - PX + 1) + abs(2 * (g % PY) - PY + 1), g),
        )
        dims = (nests, PY, PX, L, cx, cy, m, W)
        return body(dims, tuple(places[:L]), initial_state, drive_modes, relax_rates, nest_offsets)

    return jax.shard_map(
        local,
        mesh=mesh,
        in_specs=(spec, P(), P("nest", None), P()),
        out_specs=(spec, P("nest", None, None, None)),
        check_vma=False,
    )
```

time: 133 us -> 29.8 us (0.22)
  the two profiles are of different devices: /device:TPU:1 before, /device:TPU:3 now
where the time goes in v1:
time: 29.8 us; the launch traced here: 29.6 us
  Pallas kernels  25.4 us (85%)
  local copies, waits for them, and re-layouts  3.6 us (12%)
  between operations  0.65 us (2%)
    pallas_call x1, Pallas kernels, body(): pl.pallas_call(functools.partial(kernel, dims, owners), out_shape=(jax.Sh...  25.4 us
    unnamed x5, local copies, waits for them, and re-layouts  3.6 us

profile of v1, /device:TPU:3, one launch (start us, length us, event | category | flops | bytes accessed | tf_op | source)
XLA Modules:
  0.0 29.6 jit_solution(13502939968338282959)
XLA Ops:
  0.6 1.3 %copy.11.offs = s32[4,2]{1,0:T(4,128)} copy(s32[4,2]{0,1:T(2,128)} %param.12) | data formatting | bytes 64 | tf_op args[3]
  2.0 25.4 %shard_map.104 = (f32[1,4,64,128]{3,2,1,0:T(8,128)}, f32[1,4,64,64]{3,2,1,0:T(8,128)}) custom-call(f32[1,4,64,128]{3,2,1,0:T(8,128)} %field.1, f32[3,4,64,64]{3,2,1,0:T(8,128)} %drive.1, f32[1,4]{1,0:T(1,128)} %relax.1, s32[4,2]{1,0:T(4,128)} %copy.11.offs, bf16[2,256,192]{2,1,0:T(8,128)(2,1)} %constant.10.clone.u_hbm, ...), custom_call_target="tpu_custom_call" | custom-call | tf_op jit(solution)/shard_map/pallas_call | solution.py:391
  27.4 0.0 copy-start
  27.4 1.6 %copy.14 = f32[1,4,64,128]{3,2,1,0:T(8,128)} copy(f32[1,4,64,128]{3,2,1,0:T(8,128)} %get-tuple-element.4) | data formatting | bytes 262144
  29.0 0.0 copy-done
  29.0 0.7 %copy.15 = f32[1,4,64,64]{3,2,1,0:T(8,128)} copy(f32[1,4,64,64]{3,2,1,0:T(8,128)S(1)} %copy-done) | data formatting | bytes 131072
Async XLA Ops:
  27.4 1.6 %copy-start = (f32[1,4,64,64]{3,2,1,0:T(8,128)S(1)}, f32[1,4,64,64]{3,2,1,0:T(8,128)}, u32[]{:S(2)}) copy-start(f32[1,4,64,64]{3,2,1,0:T(8,128)} %get-tuple-element.5) | copy-start | bytes 196612

commit v2 on v1

--- a/solution.py
+++ b/solution.py
@@ -56,6 +56,16 @@
     return mm(a[0], b[0]) + (mm(a[0], b[1]) + mm(a[1], b[0]))
 
 
+def pack(x):
+    h = x.shape[0] // 2
+    return jnp.concatenate([x[:h], x[h:]], 1)
+
+
+def unpack(x):
+    h = x.shape[1] // 2
+    return jnp.concatenate([x[:, :h], x[:, h:]], 0)
+
+
 def loop(n, fn):
     if n <= 16:
         for i in range(n):
@@ -68,8 +78,9 @@
     dims, owners,
     field, drive, relax, offs, u_hbm, ut_hbm, v_hbm, vt_hbm, small_hbm,
     out, modes,
-    fvm, fbuf, gbuf, fin, par, cbuf, tx, u_t, ut_t, v_t, vt_t, small,
-    load_sem, a_send, a_recv, c_send, c_recv, f_send, f_recv, m_send, m_recv,
+    fvm, fbuf, gbuf, fin, start, par, cbuf, sib, obuf, lead, glead, mbuf, tx,
+    u_t, ut_t, v_t, vt_t, small,
+    load_sem, a_send, a_recv, c_send, c_recv, o_sem, g_sem, f_send, f_recv, m_send, m_recv,
 ):
     nests, PY, PX, L, cx, cy, m, W = dims
     G, nx, ny = PY * PX, cx * PX, cy * PY
@@ -85,6 +96,13 @@
     def plain(g):
         return functools.reduce(jnp.logical_and, [g != o for o in owners])
 
+    odd = k % 2 == 1
+    hops = [
+        (-1, k > 0),
+        (1, k < nests - 1),
+        (-2, jnp.logical_and(odd, k > 2)),
+        (2, jnp.logical_and(odd, k < nests - 2)),
+    ]
     barrier = pltpu.get_barrier_semaphore()
     for l, o in enumerate(owners):
         @pl.when(me != o)
@@ -99,13 +117,25 @@
                 pl.semaphore_signal(barrier, inc=1, device_id=at(g), device_id_type=MESH)
         loop(G, greet)
 
-        @pl.when(k > 0)
-        def _():
-            pl.semaphore_signal(barrier, inc=1, device_id=(k - 1, py, px), device_id_type=MESH)
-
-        @pl.when(k < nests - 1)
-        def _():
-            pl.semaphore_signal(barrier, inc=1, device_id=(k + 1, py, px), device_id_type=MESH)
+        for hop, cond in hops:
+            @pl.when(cond)
+            def _():
+                pl.semaphore_signal(
+                    barrier, inc=1, device_id=(k + hop, py, px), device_id_type=MESH
+                )
+
+    def hop_copy(src, dst, send_sem, recv_sem, hop):
+        return pltpu.make_async_remote_copy(
+            src_ref=src, dst_ref=dst, send_sem=send_sem, recv_sem=recv_sem,
+            device_id=(k + hop, py, px), device_id_type=MESH,
+        )
+
+    gain_out = hop_copy(lead, glead, g_sem.at[0], g_sem.at[1], 1)
+    gain_in = hop_copy(lead, glead, g_sem.at[0], g_sem.at[1], -1)
+    own_out_copy = hop_copy(obuf, sib, o_sem.at[0], o_sem.at[1], 1)
+    own_in = hop_copy(obuf, sib, o_sem.at[0], o_sem.at[1], -1)
+    chain_out = [hop_copy(cbuf, par, c_send.at[h - 1], c_recv, h) for h in (1, 2)]
+    chain_in = hop_copy(cbuf, par, c_send.at[0], c_recv, -1)
 
     loads = [pltpu.make_async_copy(field.at[0, l], fvm.at[l], load_sem.at[l]) for l in range(L)]
     for c in loads:
@@ -116,20 +146,18 @@
             [(v_hbm, v_t), (ut_hbm, ut_t), (small_hbm, small), (u_hbm, u_t), (vt_hbm, vt_t)]
         )
     ]
-    get_drive = pltpu.make_async_copy(drive.at[:, level], par, load_sem.at[L + 5])
+    get_drive = pltpu.make_async_copy(drive.at[:, level], start, load_sem.at[L + 5])
 
     @pl.when(is_owner)
     def _():
         for c in tables:
             c.start()
 
-        @pl.when(k == 0)
+        @pl.when(k < 2)
         def _():
             get_drive.start()
 
-        pl.semaphore_wait(
-            barrier, G - 1 + jnp.where(k > 0, 1, 0) + jnp.where(k < nests - 1, 1, 0)
-        )
+        pl.semaphore_wait(barrier, G - 1 + sum(jnp.where(c, 1, 0) for _, c in hops))
 
     @pl.when(jnp.logical_not(is_owner))
     def _():
@@ -167,48 +195,84 @@
         for ref in (fbuf, gbuf):
             ref[0:8, :] = edge
             ref[nx + 8 : nx + 16, :] = edge
+        gain = relax[0, level]
+        lead[...] = jnp.full(lead.shape, gain, F32)
+
+        @pl.when(jnp.logical_and(jnp.logical_not(odd), k < nests - 1))
+        def _():
+            gain_out.start()
+
         tables[2].wait()
-        gain = relax[0, level]
-        rest = 2.0 * (1.0 - gain)
-
-        def turn(cells, dim, axis):
+
+        def turn(kk, cells, dim, axis):
             number = lax.broadcasted_iota(jnp.int32, (m, m), dim).astype(F32)
-            product = number * (2 * RATIO * offs[k, axis]).astype(F32)
+            product = number * (2 * RATIO * offs[axis, kk]).astype(F32)
             period = float(4 * RATIO * cells)
             product = product - period * jnp.floor(product * (1.0 / period))
             angle = product * (math.pi / (2.0 * RATIO * cells))
             return jnp.cos(angle), jnp.sin(angle)
 
-        eye = jnp.where(
-            lax.broadcasted_iota(jnp.int32, (m, m), 0) == lax.broadcasted_iota(jnp.int32, (m, m), 1),
-            1.0, 0.0,
-        ).astype(F32)
-        cos_x, sin_x = turn(nx, 1, 0)
-        cos_y, sin_y = turn(ny, 0, 1)
-        row = jnp.where(k == 0, eye, small[0] * cos_x - small[1] * sin_x)
-        col = jnp.where(k == 0, eye, small[2] * cos_y - small[3] * sin_y)
+        def flat(kk):
+            eye = jnp.where(
+                lax.broadcasted_iota(jnp.int32, (m, m), 0)
+                == lax.broadcasted_iota(jnp.int32, (m, m), 1),
+                1.0, 0.0,
+            ).astype(F32)
+            cos_x, sin_x = turn(kk, nx, 1, 0)
+            cos_y, sin_y = turn(kk, ny, 0, 1)
+            row = jnp.where(kk == 0, eye, small[0] * cos_x - small[1] * sin_x)
+            col = jnp.where(kk == 0, eye, small[2] * cos_y - small[3] * sin_y)
+            return split(row), split(col)
+
         a1, b1 = split(small[4]), split(small[7])
-        a2 = split(small[5] - gain * small[6])
-        b2 = split(small[8] - gain * small[9])
-        f0, g0 = split(row), split(col)
-        f1, f2 = split(dot3(a1, f0)), split(dot3(a2, f0))
-        g1, g2 = split(dot3(g0, b1)), split(dot3(g0, b2))
-
-        def follow():
-            c1, c2, c3 = (split(par[w]) for w in range(W))
+
+        def curved(rate):
+            return split(small[5] - rate * small[6]), split(small[8] - rate * small[9])
+
+        def maps(kk, rate):
+            a2, b2 = curved(rate)
+            f0, g0 = flat(kk)
+            f1, f2 = split(dot3(a1, f0)), split(dot3(a2, f0))
+            g1, g2 = split(dot3(g0, b1)), split(dot3(g0, b2))
+            return f0, f1, f2, g0, g1, g2, 2.0 * (1.0 - rate)
+
+        def follow(cs, ms):
+            f0, f1, f2, g0, g1, g2, rest = ms
+            c1, c2, c3 = (split(c) for c in cs)
             y10, y20, y30 = dot3(c1, g0), dot3(c2, g0), dot3(c3, g0)
             y11, y21, y12 = dot3(c1, g1), dot3(c2, g1), dot3(c1, g2)
             y10s = split(y10)
-            tx[0] = dot3(f0, y10s)
-            tx[1] = dot3(f0, y20)
-            tx[2] = dot3(f0, y30)
-            tx[3] = dot3(f1, y10s) + dot3(f0, y11)
-            tx[4] = dot3(f0, y21 + y12) + dot3(f1, y20 + rest * y11) + dot3(f2, y10s)
-
-        @pl.when(k == 0)
+            return (
+                dot3(f0, y10s),
+                dot3(f0, y20),
+                dot3(f0, y30),
+                dot3(f1, y10s) + dot3(f0, y11),
+                dot3(f0, y21 + y12) + dot3(f1, y20 + rest * y11) + dot3(f2, y10s),
+            )
+
+        def nudge(own, moved, rate):
+            own2, own3 = own[1] + rate * moved[3], own[2] + rate * moved[4]
+            d1, d2, d3 = rate * (moved[0] - own[0]), rate * (moved[1] - own2), rate * (moved[2] - own3)
+            return (d1, d2, d3), (own[0] + d1, own2 + d2, own3 + d3)
+
+        own_maps = maps(k, gain)
+
+        @pl.when(odd)
+        def _():
+            gain_in.wait_recv()
+            lead[...] = glead[...]
+
+        lead_gain = lead[0:1, 0:m]
+        lead_maps = maps(k - k % 2, lead_gain)
+
+        def first(cs):
+            for i, x in enumerate(follow(cs, lead_maps)):
+                tx[i] = x
+
+        @pl.when(k < 2)
         def _():
             get_drive.wait()
-            follow()
+            first([start[w] for w in range(W)])
 
         tables[0].wait()
         tables[1].wait()
@@ -238,60 +302,68 @@
         s1, s2, s3 = (
             sum(float(math.comb(w, i)) * block(i, w - i) for i in range(w + 1)) for w in (1, 2, 3)
         )
+        a2, b2 = curved(gain)
         s1s, s2s = split(s1), split(s2)
         z11 = dot3(s1s, b1)
         x2 = dot3(a1, s1s) + z11
-        x3 = dot3(s2s, b1) + dot3(s1s, b2) + dot3(a1, s2 + rest * z11) + dot3(a2, s1s)
-        o2, o3 = s2 - gain * x2, s3 - gain * x3
-
-        rows = 32
+        x3 = dot3(s2s, b1) + dot3(s1s, b2) + dot3(a1, s2 + 2.0 * (1.0 - gain) * z11) + dot3(a2, s1s)
+        own = (s1, s2 - gain * x2, s3 - gain * x3)
+
+        @pl.when(jnp.logical_and(jnp.logical_not(odd), k < nests - 1))
+        def _():
+            for w in range(W):
+                obuf[w] = pack(own[w])
+            own_out_copy.start()
+
+        rows = min(64, nx)
 
         def free():
             col_id = lax.broadcasted_iota(jnp.int32, (rows, ny), 1)
 
             def sweep(src, dst):
                 def some(r, carry):
-                    start = pl.multiple_of(r * rows, 8)
-                    wide = src[pl.ds(start, rows + 16), :]
+                    at_row = pl.multiple_of(r * rows, 8)
+                    wide = src[pl.ds(at_row, rows + 16), :]
                     mid = wide[8 : rows + 8]
                     near = wide[7 : rows + 7] + wide[9 : rows + 9]
                     near = near + jnp.where(col_id == 0, 0.0, pltpu.roll(mid, 1, 1))
                     near = near + jnp.where(col_id == ny - 1, 0.0, pltpu.roll(mid, ny - 1, 1))
-                    dst[pl.ds(pl.multiple_of(start + 8, 8), rows), :] = mid + RATE * (near - 4.0 * mid)
+                    dst[pl.ds(pl.multiple_of(at_row + 8, 8), rows), :] = mid + RATE * (near - 4.0 * mid)
                     return carry
-                lax.fori_loop(0, nx // rows, some, 0)
+                lax.fori_loop(0, nx // rows, some, 0, unroll=nx // rows <= 4)
             sweep(fbuf, gbuf)
             sweep(gbuf, fbuf)
             sweep(fbuf, gbuf)
 
-        chain_in = pltpu.make_async_remote_copy(
-            src_ref=cbuf, dst_ref=par, send_sem=c_send, recv_sem=c_recv,
-            device_id=(k, py, px), device_id_type=MESH,
-        )
-        chain_out = pltpu.make_async_remote_copy(
-            src_ref=cbuf, dst_ref=par, send_sem=c_send, recv_sem=c_recv,
-            device_id=(k + 1, py, px), device_id_type=MESH,
-        )
-
         @pl.when(k > 0)
         def _():
             free()
+
+        @pl.when(k > 1)
+        def _():
             chain_in.wait_recv()
-            follow()
-
-        own2, own3 = o2 + gain * tx[3], o3 + gain * tx[4]
-        d1, d2, d3 = gain * (tx[0] - s1), gain * (tx[1] - own2), gain * (tx[2] - own3)
-        cbuf[0] = s1 + d1
-        cbuf[1] = own2 + d2
-        cbuf[2] = own3 + d3
-
-        @pl.when(k < nests - 1)
-        def _():
-            chain_out.start()
+            first([unpack(par[w]) for w in range(W)])
+
+        @pl.when(odd)
+        def _():
+            own_in.wait_recv()
+            _, above = nudge(
+                [unpack(sib[w]) for w in range(W)], [tx[i] for i in range(5)], lead_gain
+            )
+            for i, x in enumerate(follow(above, own_maps)):
+                tx[i] = x
+
+        (d1, d2, d3), now = nudge(own, [tx[i] for i in range(5)], gain)
+        for w in range(W):
+            cbuf[w] = pack(now[w])
+        for h in (1, 2):
+            @pl.when(jnp.logical_and(odd, k < nests - h))
+            def _():
+                chain_out[h - 1].start()
 
         def tell(g):
             return pltpu.make_async_remote_copy(
-                src_ref=cbuf.at[W - 1], dst_ref=modes.at[0, level], send_sem=m_send.at[g],
+                src_ref=cbuf.at[W - 1], dst_ref=mbuf.at[level], send_sem=m_send.at[g],
                 recv_sem=m_recv.at[level], device_id=at(g), device_id_type=MESH,
             )
 
@@ -300,7 +372,7 @@
             def _():
                 tell(g).start()
         loop(G, tell_start)
-        own_modes = pltpu.make_async_copy(cbuf.at[W - 1], modes.at[0, level], m_recv.at[level])
+        own_modes = pltpu.make_async_copy(cbuf.at[W - 1], mbuf.at[level], m_recv.at[level])
         own_modes.start()
 
         @pl.when(k == 0)
@@ -324,7 +396,8 @@
 
         own_out = pltpu.make_async_copy(patch(fin, me, 0), out.at[0, level], f_recv.at[level])
 
-        def finish(r):
+        def finish(i):
+            r = jnp.where(2 * px < PX, PX - 1 - i, i)
             here = pl.ds(pl.multiple_of(r * cx, 8), cx)
             there = pl.ds(pl.multiple_of(r * cx + 8, 8), cx)
             fin[here, :] = gbuf[there, :] + dot3((u_t[0, here, :], u_t[1, here, :]), mixed)
@@ -352,15 +425,21 @@
                 send_back(g).wait_send()
         loop(G, drain)
 
-        @pl.when(k < nests - 1)
-        def _():
-            chain_out.wait_send()
+        for h in (1, 2):
+            @pl.when(jnp.logical_and(odd, k < nests - h))
+            def _():
+                chain_out[h - 1].wait_send()
+
+        @pl.when(jnp.logical_and(jnp.logical_not(odd), k < nests - 1))
+        def _():
+            gain_out.wait_send()
+            own_out_copy.wait_send()
 
     for l, o in enumerate(owners):
         @pl.when(me != o)
         def _():
             pltpu.make_async_remote_copy(
-                src_ref=cbuf.at[W - 1], dst_ref=modes.at[0, l], send_sem=m_send.at[0],
+                src_ref=cbuf.at[W - 1], dst_ref=mbuf.at[l], send_sem=m_send.at[0],
                 recv_sem=m_recv.at[l], device_id=at(o), device_id_type=MESH,
             ).wait_recv()
             pltpu.make_async_remote_copy(
@@ -368,6 +447,8 @@
                 recv_sem=f_recv.at[l], device_id=at(o), device_id_type=MESH,
             ).wait_recv()
             gather(l).wait_send()
+    for l in range(L):
+        modes[0, l] = unpack(mbuf[l])
 
 
 def body(dims, owners, initial_state, drive_modes, relax_rates, nest_offsets):
@@ -391,18 +472,24 @@
     return pl.pallas_call(
         functools.partial(kernel, dims, owners),
         out_shape=(
-            jax.ShapeDtypeStruct((1, L, cx, cy), F32),
-            jax.ShapeDtypeStruct((1, L, m, m), F32),
+            pltpu.VMEM((1, L, cx, cy), F32),
+            pltpu.VMEM((1, L, m, m), F32),
         ),
         in_specs=[any_space, any_space, smem, smem] + [any_space] * 5,
-        out_specs=(vmem, vmem),
+        out_specs=(any_space, vmem),
         scratch_shapes=[
             pltpu.VMEM((L, cx, cy), F32),
             pltpu.VMEM((nx + 16, ny), F32),
             pltpu.VMEM((nx + 16, ny), F32),
             pltpu.VMEM((nx, ny), F32),
             pltpu.VMEM((W, m, m), F32),
-            pltpu.VMEM((W, m, m), F32),
+            pltpu.VMEM((W, m // 2, 2 * m), F32),
+            pltpu.VMEM((W, m // 2, 2 * m), F32),
+            pltpu.VMEM((W, m // 2, 2 * m), F32),
+            pltpu.VMEM((W, m // 2, 2 * m), F32),
+            pltpu.VMEM((8, 128), F32),
+            pltpu.VMEM((8, 128), F32),
+            pltpu.VMEM((L, m // 2, 2 * m), F32),
             pltpu.VMEM((5, m, m), F32),
             pltpu.VMEM((2, nx, wide), BF16),
             pltpu.VMEM((2, deep, nx), BF16),
@@ -412,15 +499,17 @@
             dma((L + 6,)),
             dma((L,)),
             dma((G,)),
+            dma((2,)),
             dma,
-            dma,
+            dma((2,)),
+            dma((2,)),
             dma((G,)),
             dma((L,)),
             dma((G,)),
             dma((L,)),
         ],
         compiler_params=pltpu.CompilerParams(collective_id=0, has_side_effects=True),
-    )(initial_state, drive_modes, relax_rates, nest_offsets,
+    )(initial_state, drive_modes, relax_rates, nest_offsets.T,
       *(jnp.asarray(t) for t in tables), jnp.asarray(small))
 
 

time: 29.8 us -> 24.4 us (0.82)
  Pallas kernels: 25.4 us -> 22.1 us
  local copies, waits for them, and re-layouts: 3.6 us -> 1.31 us
    pallas_call x1, Pallas kernels: 25.4 us -> 22.1 us  [body(): pl.pallas_call(functools.partial(kernel, dims, owners), out_shape=(pltpu....]
    unnamed x5 -> x2, local copies, waits for them, and re-layouts: 3.6 us -> 1.31 us
where the time goes in v2:
time: 24.4 us; the launch traced here: 24.1 us
  Pallas kernels  22.1 us (91%)
  local copies, waits for them, and re-layouts  1.31 us (5%)
  between operations  0.64 us (3%)
    pallas_call x1, Pallas kernels, body(): pl.pallas_call(functools.partial(kernel, dims, owners), out_shape=(pltpu....  22.1 us
    unnamed x2, local copies, waits for them, and re-layouts  1.31 us

profile of v2, /device:TPU:3, one launch (start us, length us, event | category | flops | bytes accessed | tf_op | source)
XLA Modules:
  0.0 24.1 jit_solution(11310698182258057159)
XLA Ops:
  0.6 22.1 %shard_map.104 = (f32[1,4,64,128]{3,2,1,0:T(8,128)S(1)}, f32[1,4,64,64]{3,2,1,0:T(8,128)S(1)}) custom-call(f32[1,4,64,128]{3,2,1,0:T(8,128)} %field.1, f32[3,4,64,64]{3,2,1,0:T(8,128)} %drive.1, f32[1,4]{1,0:T(1,128)} %relax.1, s32[2,4]{1,0:T(2,128)} %bitcast.1, bf16[2,256,192]{2,1,0:T(8,128)(2,1)} %constant.10.clone.u_hbm, ...), custom_call_target="tpu_custom_call" | custom-call | tf_op jit(solution)/shard_map/pallas_call | solution.py:472
  22.8 0.7 %copy.13 = f32[1,4,64,128]{3,2,1,0:T(8,128)} copy(f32[1,4,64,128]{3,2,1,0:T(8,128)S(1)} %get-tuple-element.2) | data formatting | bytes 262144
  23.4 0.7 %copy.14 = f32[1,4,64,64]{3,2,1,0:T(8,128)} copy(f32[1,4,64,64]{3,2,1,0:T(8,128)S(1)} %get-tuple-element.3) | data formatting | bytes 131072

commit v3 on v2

--- a/solution.py
+++ b/solution.py
@@ -76,10 +76,10 @@
 
 def kernel(
     dims, owners,
-    field, drive, relax, offs, u_hbm, ut_hbm, v_hbm, vt_hbm, small_hbm,
+    field, drive, relax_hbm, offs_hbm, u_hbm, ut_hbm, v_hbm, vt_hbm, small_hbm,
     out, modes,
     fvm, fbuf, gbuf, fin, start, par, cbuf, sib, obuf, lead, glead, mbuf, tx,
-    u_t, ut_t, v_t, vt_t, small,
+    u_t, ut_t, v_t, vt_t, small, relax, offs,
     load_sem, a_send, a_recv, c_send, c_recv, o_sem, g_sem, f_send, f_recv, m_send, m_recv,
 ):
     nests, PY, PX, L, cx, cy, m, W = dims
@@ -143,10 +143,13 @@
     tables = [
         pltpu.make_async_copy(src, dst, load_sem.at[L + i])
         for i, (src, dst) in enumerate(
-            [(v_hbm, v_t), (ut_hbm, ut_t), (small_hbm, small), (u_hbm, u_t), (vt_hbm, vt_t)]
+            [
+                (v_hbm, v_t), (ut_hbm, ut_t), (small_hbm, small), (u_hbm, u_t), (vt_hbm, vt_t),
+                (relax_hbm, relax), (offs_hbm, offs),
+            ]
         )
     ]
-    get_drive = pltpu.make_async_copy(drive.at[:, level], start, load_sem.at[L + 5])
+    get_drive = pltpu.make_async_copy(drive.at[:, level], start, load_sem.at[L + 7])
 
     @pl.when(is_owner)
     def _():
@@ -195,6 +198,8 @@
         for ref in (fbuf, gbuf):
             ref[0:8, :] = edge
             ref[nx + 8 : nx + 16, :] = edge
+        tables[5].wait()
+        tables[6].wait()
         gain = relax[0, level]
         lead[...] = jnp.full(lead.shape, gain, F32)
 
@@ -356,7 +361,7 @@
         (d1, d2, d3), now = nudge(own, [tx[i] for i in range(5)], gain)
         for w in range(W):
             cbuf[w] = pack(now[w])
-        for h in (1, 2):
+        for h in (2, 1):
             @pl.when(jnp.logical_and(odd, k < nests - h))
             def _():
                 chain_out[h - 1].start()
@@ -449,6 +454,17 @@
             gather(l).wait_send()
     for l in range(L):
         modes[0, l] = unpack(mbuf[l])
+
+
+def store(state, modes, state_out, modes_out, sem):
+    copies = [
+        pltpu.make_async_copy(state, state_out, sem.at[0]),
+        pltpu.make_async_copy(modes, modes_out, sem.at[1]),
+    ]
+    for c in copies:
+        c.start()
+    for c in copies:
+        c.wait()
 
 
 def body(dims, owners, initial_state, drive_modes, relax_rates, nest_offsets):
@@ -467,15 +483,14 @@
     tables = (halves(u[:, :wide]), halves(u.T), halves(v), halves(v.T[:wide]))
     any_space = pl.BlockSpec(memory_space=pl.ANY)
     vmem = pl.BlockSpec(memory_space=pltpu.VMEM)
-    smem = pl.BlockSpec(memory_space=pltpu.SMEM)
     dma = pltpu.SemaphoreType.DMA
-    return pl.pallas_call(
+    held = pl.pallas_call(
         functools.partial(kernel, dims, owners),
         out_shape=(
             pltpu.VMEM((1, L, cx, cy), F32),
             pltpu.VMEM((1, L, m, m), F32),
         ),
-        in_specs=[any_space, any_space, smem, smem] + [any_space] * 5,
+        in_specs=[any_space] * 9,
         out_specs=(any_space, vmem),
         scratch_shapes=[
             pltpu.VMEM((L, cx, cy), F32),
@@ -496,7 +511,9 @@
             pltpu.VMEM((2, ny, deep), BF16),
             pltpu.VMEM((2, wide, ny), BF16),
             pltpu.VMEM((10, m, m), F32),
-            dma((L + 6,)),
+            pltpu.SMEM(relax_rates.shape, F32),
+            pltpu.SMEM(nest_offsets.shape[::-1], jnp.int32),
+            dma((L + 8,)),
             dma((L,)),
             dma((G,)),
             dma((2,)),
@@ -511,6 +528,13 @@
         compiler_params=pltpu.CompilerParams(collective_id=0, has_side_effects=True),
     )(initial_state, drive_modes, relax_rates, nest_offsets.T,
       *(jnp.asarray(t) for t in tables), jnp.asarray(small))
+    return pl.pallas_call(
+        store,
+        out_shape=[jax.ShapeDtypeStruct(x.shape, F32) for x in held],
+        in_specs=[any_space] * 2,
+        out_specs=[any_space] * 2,
+        scratch_shapes=[dma((2,))],
+    )(*(pltpu.with_memory_space_constraint(x, pltpu.VMEM) for x in held))
 
 
 def solution(mesh):

time: 24.4 us -> 23.1 us (0.947)
  the two profiles are of different devices: /device:TPU:3 before, /device:TPU:2 now
where the time goes in v3:
time: 23.1 us; the launch traced here: 23 us
  Pallas kernels  22.3 us (97%)
  between operations  0.64 us (3%)
    pallas_call x1, Pallas kernels, body(): pl.pallas_call(functools.partial(kernel, dims, owners), out_shape=(pltpu....  21.6 us
    pallas_call x1, Pallas kernels, body(): pl.pallas_call(store, out_shape=[jax.ShapeDtypeStruct(x.shape, F32) for x...  0.72 us

profile of v3, /device:TPU:2, one launch (start us, length us, event | category | flops | bytes accessed | tf_op | source)
XLA Modules:
  0.0 23.0 jit_solution(11799546901750403612)
XLA Ops:
  0.6 21.6 %shard_map.104 = (f32[1,4,64,128]{3,2,1,0:T(8,128)S(1)}, f32[1,4,64,64]{3,2,1,0:T(8,128)S(1)}) custom-call(f32[1,4,64,128]{3,2,1,0:T(8,128)} %field.1, f32[3,4,64,64]{3,2,1,0:T(8,128)} %drive.1, f32[1,4]{1,0:T(1,128)} %relax_hbm.1, s32[2,4]{1,0:T(2,128)} %bitcast.1, bf16[2,256,192]{2,1,0:T(8,128)(2,1)} %constant.10.clone.u_hbm, ...), custom_call_target="tpu_custom_call" | custom-call | tf_op jit(solution)/shard_map/pallas_call | solution.py:487
  22.2 0.7 %shard_map.105 = (f32[1,4,64,128]{3,2,1,0:T(8,128)}, f32[1,4,64,64]{3,2,1,0:T(8,128)}) custom-call(f32[1,4,64,128]{3,2,1,0:T(8,128)S(1)} %get-tuple-element.4.state, f32[1,4,64,64]{3,2,1,0:T(8,128)S(1)} %get-tuple-element.5.modes), custom_call_target="tpu_custom_call" | custom-call | tf_op jit(solution)/shard_map/pallas_call | solution.py:531

commit v4 on v2

v4 whole, which is shorter than its diff:
```python
import functools
import math

import jax
import jax.numpy as jnp
import numpy as np
from jax import lax
from jax.experimental import pallas as pl
from jax.experimental.pallas import tpu as pltpu
from jax.sharding import PartitionSpec as P

RATIO = 3
RATE = 0.2
MESH = pl.DeviceIdType.MESH
F32, BF16 = jnp.float32, jnp.bfloat16


def basis(cells, modes, refine, fn=np.cos):
    j = np.arange(modes, dtype=np.int64)
    q = 2 * np.arange(cells, dtype=np.int64) + 1
    product = (j[None, :] * q[:, None]) % (4 * refine * cells)
    weight = np.where(j == 0, 1.0, 2.0) / cells
    return np.sqrt(weight)[None, :] * fn(np.pi * product / (2.0 * refine * cells))


def half_step(table):
    pad = np.pad(table, ((1, 1), (0, 0)))
    return (0.5 - 2 * RATE) * table + RATE * (pad[2:] + pad[:-2])


def powers(table, count):
    out = [table]
    for _ in range(count):
        out.append(half_step(out[-1]))
    return out


def halves(table):
    high = np.asarray(table, np.float32).astype(BF16)
    low = (np.asarray(table, np.float64) - high.astype(np.float64)).astype(np.float32)
    return np.stack([high, low.astype(BF16)])


def split(x):
    high = x.astype(BF16)
    return high, (x - high.astype(F32)).astype(BF16)


def mm(a, b):
    return lax.dot_general(a, b, (((1,), (0,)), ((), ())), preferred_element_type=F32)


def dot3(a, b):
    a = a if isinstance(a, tuple) else split(a)
    b = b if isinstance(b, tuple) else split(b)
    return mm(a[0], b[0]) + (mm(a[0], b[1]) + mm(a[1], b[0]))


def dot3t(a, b):
    b = b if isinstance(b, tuple) else split(b)

    def nt(x, y):
        return lax.dot_general(x, y, (((1,), (1,)), ((), ())), preferred_element_type=F32)

    return nt(a[0], b[0]) + (nt(a[0], b[1]) + nt(a[1], b[0]))


def pack(x):
    h = x.shape[0] // 2
    return jnp.concatenate([x[:h], x[h:]], 1)


def unpack(x):
    h = x.shape[1] // 2
    return jnp.concatenate([x[:, :h], x[:, h:]], 0)


def pack_wide(x, m):
    low = x[:m].T[m : m + 8]
    return jnp.concatenate(
        [pack(x[:m, :m]), x[m : m + 8], jnp.concatenate([low, jnp.zeros_like(low)], 1)], 0
    )


def unpack_fix(x, m):
    tile = x[m // 2 :]
    low = jnp.concatenate([tile[:, :m], jnp.zeros((m - 8, m), F32)], 0).T
    top = jnp.concatenate([unpack(x[: m // 2]), low], 1)
    return jnp.concatenate([top, tile, jnp.zeros((8, 2 * m), F32)], 0)[:, : m + 16]


def unpack_wide(x, m):
    low = jnp.concatenate([x[m // 2 + 8 :, :m], jnp.zeros((m - 8, m), F32)], 0).T
    top = jnp.concatenate([unpack(x[: m // 2]), low], 1)
    return jnp.concatenate([top, x[m // 2 : m // 2 + 8], jnp.zeros((8, 2 * m), F32)], 0)


def loop(n, fn):
    if n <= 16:
        for i in range(n):
            fn(i)
    else:
        lax.fori_loop(0, n, lambda i, c: (fn(i), c)[1], 0)


def kernel(
    dims, owners,
    field, drive, relax_hbm, offs_hbm,
    u_hbm, ut_hbm, v_hbm, vt_hbm, left_hbm, right_hbm, up_hbm, down_hbm, small_hbm,
    out, modes,
    fvm, pbuf, abuf, strip, near, wide, calm, state, fix, u_t, vt_t, zbuf, mail, start, par, cbuf, lead, glead, tx,
    ut_t, v_t, left, right, up, down, small, relax, offs,
    load_sem, a_send, a_recv, h_send, h_recv, c_sem, g_sem, out_sem, f_send, f_recv, m_send, m_recv,
):
    nests, PY, PX, L, cx, cy, m, W = dims
    G, nx, ny = PY * PX, cx * PX, cy * PY
    k, py, px = lax.axis_index("nest"), lax.axis_index("py"), lax.axis_index("px")
    me = px * PY + py
    odd = k % 2 == 1
    leader = k + 1 - k % 2
    placed = [me == o for o in owners]
    level = sum(jnp.where(c, l, 0) for l, c in enumerate(placed))
    in_place = functools.reduce(jnp.logical_or, placed)
    is_owner = jnp.logical_and(odd, in_place)
    is_spare = jnp.logical_and(jnp.logical_not(odd), in_place)
    owns = [jnp.logical_and(odd, c) for c in placed]

    def at(g, nest):
        return (nest, g % PY, g // PY)

    def plain(g):
        return functools.reduce(jnp.logical_and, [g != o for o in owners])

    hops = [(-2, k > 2), (2, k < nests - 2)]
    sides = [
        (px > 0, (k, py, px - 1)), (px < PX - 1, (k, py, px + 1)),
        (py > 0, (k, py - 1, px)), (py < PY - 1, (k, py + 1, px)),
    ]
    beside = sum(jnp.where(c, 1, 0) for c, _ in sides)
    barrier = pltpu.get_barrier_semaphore()
    for l, o in enumerate(owners):
        @pl.when(jnp.logical_not(owns[l]))
        def _():
            pl.semaphore_signal(barrier, inc=1, device_id=at(o, leader), device_id_type=MESH)

    for cond, device in sides:
        @pl.when(cond)
        def _():
            pl.semaphore_signal(barrier, inc=1, device_id=device, device_id_type=MESH)

    @pl.when(is_owner)
    def _():
        def greet(g):
            pl.semaphore_signal(barrier, inc=1, device_id=at(g, k - 1), device_id_type=MESH)

            @pl.when(plain(g))
            def _():
                pl.semaphore_signal(barrier, inc=1, device_id=at(g, k), device_id_type=MESH)
        loop(G, greet)

        for hop, cond in hops:
            @pl.when(cond)
            def _():
                pl.semaphore_signal(
                    barrier, inc=1, device_id=(k + hop, py, px), device_id_type=MESH
                )

    def hop_copy(src, dst, send_sem, recv_sem, hop):
        return pltpu.make_async_remote_copy(
            src_ref=src, dst_ref=dst, send_sem=send_sem, recv_sem=recv_sem,
            device_id=(k + hop, py, px), device_id_type=MESH,
        )

    gain_out = hop_copy(lead, glead, g_sem.at[0], g_sem.at[1], 1)
    gain_in = hop_copy(lead, glead, g_sem.at[0], g_sem.at[1], -1)
    chain_out = hop_copy(cbuf, par, c_sem.at[0], c_sem.at[1], 2)
    chain_in = hop_copy(cbuf, par, c_sem.at[0], c_sem.at[1], -2)

    loads = [pltpu.make_async_copy(field.at[0, l], fvm.at[l], load_sem.at[l]) for l in range(L)]
    for c in loads:
        c.start()
    rows_here = pl.ds(pl.multiple_of(px * cx, 8), cx)
    cols_here = pl.ds(pl.multiple_of(py * cy, 128), cy)
    pairs = [
        (v_hbm.at[:, cols_here], v_t), (ut_hbm.at[:, px], ut_t),
        (u_hbm.at[:, rows_here], u_t), (vt_hbm.at[:, :, cols_here], vt_t),
        (relax_hbm, relax), (offs_hbm, offs), (small_hbm, small),
        (left_hbm, left), (right_hbm, right), (up_hbm, up), (down_hbm, down),
    ]
    tables = [
        pltpu.make_async_copy(src, dst, load_sem.at[L + 1 + i]) for i, (src, dst) in enumerate(pairs)
    ]
    for c in tables[:4]:
        c.start()
    get_drive = pltpu.make_async_copy(drive.at[:, level], start, load_sem.at[L])

    @pl.when(in_place)
    def _():
        tables[4].start()

    @pl.when(is_owner)
    def _():
        for c in tables[5:]:
            c.start()

        @pl.when(k < 2)
        def _():
            get_drive.start()

    tables[0].wait()
    tables[1].wait()
    for c in loads:
        c.wait()
    half = dot3(fvm[...].reshape(L * cx, cy), (v_t[0], v_t[1]))
    for l in range(L):
        pbuf[l] = pack_wide(dot3((ut_t[0], ut_t[1]), half[l * cx : (l + 1) * cx]), m)

    lane = lax.broadcasted_iota(jnp.int32, (cx, 128), 1)
    edge = jnp.zeros((cx, 128), F32)
    for l in range(L):
        ends = jnp.where(lane < 64, fvm[l, :, 0:128], fvm[l, :, cy - 128 : cy])
        turned = pltpu.roll(ends, 8 * l, 1) if l else ends
        shift = (lane - 8 * l + 4) % 128
        edge = jnp.where(shift < 8, turned, edge)
        wide[l, 8 : cx + 8, 0:cy] = fvm[l]
    folds = 128 // (8 * L)
    thin = cx // folds
    short = lax.broadcasted_iota(jnp.int32, (thin, 128), 1)
    folded = edge[:thin]
    for i in range(1, folds):
        moved = pltpu.roll(edge[i * thin : (i + 1) * thin], 8 * L * i, 1)
        folded = jnp.where((short + 4) % 128 < 8 * L * i, folded, moved)
    strip[...] = folded
    bare = jnp.zeros((8, cy + 128), F32)

    @pl.when(px == 0)
    def _():
        for l in range(L):
            wide[l, 0:8, :] = bare

    @pl.when(px == PX - 1)
    def _():
        for l in range(L):
            wide[l, cx + 8 : cx + 16, :] = bare

    @pl.when(py == 0)
    def _():
        near[0] = jnp.zeros(near.shape[1:], F32)

    @pl.when(py == PY - 1)
    def _():
        near[1] = jnp.zeros(near.shape[1:], F32)

    @pl.when(is_owner)
    def _():
        abuf[1, me] = pbuf[level]
        pl.semaphore_wait(barrier, beside + 2 * G - 1 + sum(jnp.where(c, 1, 0) for _, c in hops))

    @pl.when(jnp.logical_not(is_owner))
    def _():
        pl.semaphore_wait(barrier, beside + L)

    def remote(src, dst, send_sem, recv_sem, g, nest):
        return pltpu.make_async_remote_copy(
            src_ref=src, dst_ref=dst, send_sem=send_sem, recv_sem=recv_sem,
            device_id=at(g, nest), device_id_type=MESH,
        )

    def share(l):
        return remote(
            pbuf.at[l], abuf.at[k % 2, me], a_send.at[l], a_recv.at[k % 2, me], owners[l], leader
        )

    keep_modes = pltpu.make_async_copy(mail.at[1], modes.at[level], m_recv.at[level])

    def beam(src, dst, i, device):
        return pltpu.make_async_remote_copy(
            src_ref=src, dst_ref=dst, send_sem=h_send.at[i], recv_sem=h_recv.at[i],
            device_id=device, device_id_type=MESH,
        )

    top, bottom = pl.ds(0, 8), pl.ds(cx + 8, 8)
    first_rows, last_rows = pl.ds(8, 8), pl.ds(cx, 8)
    halo = [
        beam(wide.at[:, first_rows], wide.at[:, bottom], 0, sides[0][1]),
        beam(wide.at[:, last_rows], wide.at[:, top], 1, sides[1][1]),
        beam(strip, near.at[1], 2, sides[2][1]),
        beam(strip, near.at[0], 3, sides[3][1]),
    ]

    def start_halo(i):
        @pl.when(sides[i][0])
        def _():
            halo[i].start()

    def land_halo(i):
        @pl.when(sides[i ^ 1][0])
        def _():
            halo[i].wait_recv()

    for l, o in enumerate(owners):
        @pl.when(jnp.logical_not(owns[l]))
        def _():
            share(l).start()

    @pl.when(is_spare)
    def _():
        tables[4].wait()
        lead[...] = jnp.full(lead.shape, relax[0, level], F32)
        gain_out.start()

    start_halo(2)
    start_halo(3)

    def widen_patch():
        land_halo(2)
        land_halo(3)
        after, before = near[1], near[0]
        for l in range(L):
            for i in range(folds):
                back = (128 - 8 * l - 8 * L * i) % 128
                right, left_side = after, before
                if back:
                    right, left_side = pltpu.roll(after, back, 1), pltpu.roll(before, back, 1)
                wide[l, 8 + i * thin : 8 + (i + 1) * thin, cy:] = jnp.where(
                    short < 64, right, left_side
                )
        start_halo(0)
        start_halo(1)

    def run_free():
        land_halo(0)
        land_halo(1)
        shape = (cx + 16, cy + 128)
        row = lax.broadcasted_iota(jnp.int32, shape, 0) + (px * cx - 8)
        col = lax.broadcasted_iota(jnp.int32, shape, 1)
        col = jnp.where(col < cy + 64, col, col - (cy + 128)) + py * cy
        inside = (row >= 0) & (row < nx) & (col >= 0) & (col < ny)
        for l in range(L):
            now = wide[l]
            for _ in range(W):
                side = pltpu.roll(now, 1, 0) + pltpu.roll(now, cx + 15, 0)
                side = side + pltpu.roll(now, 1, 1) + pltpu.roll(now, cy + 127, 1)
                now = jnp.where(inside, now + RATE * (side - 4.0 * now), 0.0)
            calm[l] = now[8 : cx + 8, 0:cy]

    @pl.when(is_owner)
    def _():
        tables[4].wait()
        tables[5].wait()
        tables[6].wait()
        gain = relax[0, level]

        def turn(kk, cells, dim, axis):
            number = lax.broadcasted_iota(jnp.int32, (m, m), dim).astype(F32)
            product = number * (2 * RATIO * offs[axis, kk]).astype(F32)
            period = float(4 * RATIO * cells)
            product = product - period * jnp.floor(product * (1.0 / period))
            angle = product * (math.pi / (2.0 * RATIO * cells))
            return jnp.cos(angle), jnp.sin(angle)

        def flat(kk):
            eye = jnp.where(
                lax.broadcasted_iota(jnp.int32, (m, m), 0)
                == lax.broadcasted_iota(jnp.int32, (m, m), 1),
                1.0, 0.0,
            ).astype(F32)
            cos_x, sin_x = turn(kk, nx, 1, 0)
            cos_y, sin_y = turn(kk, ny, 0, 1)
            row = jnp.where(kk == 0, eye, small[0] * cos_x - small[1] * sin_x)
            col = jnp.where(kk == 0, eye, small[2] * cos_y - small[3] * sin_y)
            return split(row), split(col)

        a1, b1 = split(small[4]), split(small[7])

        def curved(rate):
            return split(small[5] - rate * small[6]), split(small[8] - rate * small[9])

        def maps(kk, rate):
            a2, b2 = curved(rate)
            f0, g0 = flat(kk)
            f1, f2 = split(dot3(a1, f0)), split(dot3(a2, f0))
            g1, g2 = split(dot3(g0, b1)), split(dot3(g0, b2))
            return f0, f1, f2, g0, g1, g2, 2.0 * (1.0 - rate)

        def follow(cs, ms):
            f0, f1, f2, g0, g1, g2, rest = ms
            c1, c2, c3 = (split(c) for c in cs)
            y10, y20, y30 = dot3(c1, g0), dot3(c2, g0), dot3(c3, g0)
            y11, y21, y12 = dot3(c1, g1), dot3(c2, g1), dot3(c1, g2)
            y10s = split(y10)
            return (
                dot3(f0, y10s),
                dot3(f0, y20),
                dot3(f0, y30),
                dot3(f1, y10s) + dot3(f0, y11),
                dot3(f0, y21 + y12) + dot3(f1, y20 + rest * y11) + dot3(f2, y10s),
            )

        def nudge(own, moved, rate):
            own2, own3 = own[1] + rate * moved[3], own[2] + rate * moved[4]
            d1, d2, d3 = rate * (moved[0] - own[0]), rate * (moved[1] - own2), rate * (moved[2] - own3)
            return (d1, d2, d3), (own[0] + d1, own2 + d2, own3 + d3)

        own_maps = maps(k, gain)
        gain_in.wait_recv()
        lead_gain = glead[0:1, 0:m]
        lead_maps = maps(k - 1, lead_gain)

        def first(cs):
            for i, x in enumerate(follow(cs, lead_maps)):
                tx[i] = x

        @pl.when(k < 2)
        def _():
            get_drive.wait()
            first([start[w] for w in range(W)])

        tables[7].wait()
        tables[8].wait()

        def arrive(g):
            remote(pbuf.at[0], abuf.at[0, g], a_send.at[0], a_recv.at[0, g], g, k - 1).wait_recv()

            @pl.when(g != me)
            def _():
                remote(pbuf.at[0], abuf.at[1, g], a_send.at[0], a_recv.at[1, g], g, k).wait_recv()
        loop(G, arrive)

        def project(i):
            total = abuf[i, 0]
            if G <= 16:
                for g in range(1, G):
                    total = total + abuf[i, g]
            else:
                total = lax.fori_loop(1, G, lambda g, c: c + abuf[i, g], total)
            both = dot3((left[0], left[1]), dot3(unpack_wide(total, m), (right[0], right[1])))

            def block(i, j):
                return both[i * m : (i + 1) * m, j * m : (j + 1) * m]

            return [
                sum(float(math.comb(w, i)) * block(i, w - i) for i in range(w + 1))
                for w in (1, 2, 3)
            ]

        def settle(s, rate):
            s1, s2, s3 = s
            a2, b2 = curved(rate)
            s1s, s2s = split(s1), split(s2)
            z11 = dot3(s1s, b1)
            x2 = dot3(a1, s1s) + z11
            x3 = dot3(s2s, b1) + dot3(s1s, b2) + dot3(a2, s1s)
            x3 = x3 + dot3(a1, s2 + 2.0 * (1.0 - rate) * z11)
            return s1, s2 - rate * x2, s3 - rate * x3

        before, after = project(0), project(1)
        before, after = settle(before, lead_gain), settle(after, gain)

        @pl.when(k > 1)
        def _():
            widen_patch()
            chain_in.wait_recv()
            first([unpack(par[w]) for w in range(W)])

        d_lead, c_lead = nudge(before, [tx[i] for i in range(5)], lead_gain)
        d_own, c_own = nudge(after, follow(c_lead, own_maps), gain)
        for w in range(W):
            cbuf[w] = pack(c_own[w])

        @pl.when(k < nests - 2)
        def _():
            chain_out.start()

        @pl.when(k < 2)
        def _():
            widen_patch()

        tables[9].wait()
        tables[10].wait()
        def widen(x):
            return jnp.concatenate([x, jnp.zeros_like(x)], 1)

        def table(i):
            return up[0, 16 * i : 16 * (i + 1)], up[1, 16 * i : 16 * (i + 1)]

        def correct(d):
            d1, d2, d3 = d
            e1 = split(d1)
            main = d3 + small[10] * d2 + small[11] * d1
            rows = dot3(table(0), d2 + small[12] * d1) + dot3(table(1), e1)
            cols = dot3t(table(2), d2 + small[13] * d1) + dot3t(table(3), e1)
            corner = dot3(dot3(table(0), e1), (down[0], down[1]))
            return jnp.concatenate([pack(main), (widen(rows + cols) + corner)[:8]], 0)

        zbuf[0] = correct(d_lead)
        mail[0] = pack(c_lead[W - 1])
        zbuf[1] = correct(d_own)
        mail[1] = pack(c_own[W - 1])

        def mend(i, g):
            return remote(
                zbuf.at[i], fix.at[level], f_send.at[i, g], f_recv.at[level], g, k - 1 + i
            )

        def tell(i, g):
            return remote(
                mail.at[i], modes.at[level], m_send.at[i, g], m_recv.at[level], g, k - 1 + i
            )

        for copy in (mend, tell):
            for i in range(2):
                def one(j):
                    g = jnp.where(2 * px < PX, G - 1 - j, j)

                    @pl.when(jnp.logical_or(i == 0, g != me))
                    def _():
                        copy(i, g).start()
                loop(G, one)
        fix[level] = zbuf[1]
        keep_modes.start()
        run_free()

    @pl.when(jnp.logical_not(is_owner))
    def _():
        widen_patch()
        run_free()

    tables[2].wait()
    tables[3].wait()

    puts = [pltpu.make_async_copy(state.at[l], out.at[l], out_sem.at[l]) for l in range(L)]

    def finish(some):
        for l in some:
            @pl.when(jnp.logical_not(owns[l]))
            def _():
                remote(
                    zbuf.at[0], fix.at[l], f_send.at[0, 0], f_recv.at[l], owners[l], leader
                ).wait_recv()
        half = [dot3(unpack_fix(fix[l], m), (vt_t[0], vt_t[1])) for l in some]
        for l, x in zip(some, half):
            state[l] = calm[l] + dot3((u_t[0], u_t[1]), x)
            puts[l].start()

    finish(range(L // 2))
    finish(range(L // 2, L))
    for l, o in enumerate(owners):
        @pl.when(jnp.logical_not(owns[l]))
        def _():
            remote(
                mail.at[0], modes.at[l], m_send.at[0, 0], m_recv.at[l], o, leader
            ).wait_recv()
            share(l).wait_send()

    @pl.when(is_owner)
    def _():
        keep_modes.wait()

        def drain(g):
            for i in range(2):
                @pl.when(jnp.logical_or(i == 0, g != me))
                def _():
                    remote(
                        mail.at[i], modes.at[0], m_send.at[i, g], m_recv.at[0], g, k - 1 + i
                    ).wait_send()
                    remote(
                        zbuf.at[i], fix.at[0], f_send.at[i, g], f_recv.at[0], g, k - 1 + i
                    ).wait_send()
        loop(G, drain)

        @pl.when(k < nests - 2)
        def _():
            chain_out.wait_send()

    @pl.when(is_spare)
    def _():
        gain_out.wait_send()

    for i in range(4):
        @pl.when(sides[i][0])
        def _():
            halo[i].wait_send()
    for c in puts:
        c.wait()


def store(state, packed, state_out, modes_out, modes, sem):
    first = pltpu.make_async_copy(state, state_out.at[0], sem.at[0])
    second = pltpu.make_async_copy(modes, modes_out.at[0], sem.at[1])
    first.start()
    for l in range(packed.shape[0]):
        modes[l] = unpack(packed[l])
    second.start()
    first.wait()
    second.wait()


def wide_tables(cells, modes, windows):
    stages = powers(basis(cells, modes, 1), windows)
    edges = np.zeros((cells, modes))
    for e in range(windows):
        edges[e, 2 * e] = 1.0
        edges[cells - 1 - e, 2 * e + 1] = 1.0
    full = np.concatenate([stages[0], edges], 1)
    rate = 0.5 - 2 * RATE + 2 * RATE * np.cos(np.pi * np.arange(modes) / cells)
    turns = []
    for i, t in enumerate(stages):
        top = np.diag(rate**i)
        turns.append(np.concatenate([top, edges.T @ (t - stages[0] @ top)], 0))
    return stages, full, turns, rate


def body(dims, owners, initial_state, drive_modes, relax_rates, nest_offsets):
    nests, PY, PX, L, cx, cy, m, W = dims
    G, nx, ny = PY * PX, cx * PX, cy * PY
    assert nests % 2 == 0 and W == 3
    tall, lanes = m + 16, 2 * m
    rp, u, tu, rate_x = wide_tables(nx, m, W)
    cp, v, tv, rate_y = wide_tables(ny, m, W)
    few = 2 * (W - 1)
    u_few, v_few = u[:, :tall].copy(), np.zeros((ny, tall))
    u_few[:, m + few :] = 0.0
    v_few[:, :m] = v[:, :m]
    v_few[:, m + 4 : m + 4 + few] = v[:, m : m + few]
    both = rate_x[:, None] + rate_y[None, :]
    ends = np.zeros((4, 16, m))
    ends[0, :few], ends[1, :few] = tu[1][m : m + few], tu[2][m : m + few]
    ends[2, 4 : 4 + few], ends[3, 4 : 4 + few] = tv[1][m : m + few], tv[2][m : m + few]
    corner = np.zeros((m, lanes))
    corner[:, m + 4 : m + 4 + few] = 2.0 * tv[1][m : m + few].T
    a = [rp[0].T @ t for t in rp]
    b = [cp[0].T @ t for t in cp]
    even_x, odd_x = (rp[0].T @ basis(nx, m, RATIO, f) for f in (np.cos, np.sin))
    even_y, odd_y = ((cp[0].T @ basis(ny, m, RATIO, f)).T for f in (np.cos, np.sin))
    small = np.stack(
        [even_x, odd_x, even_y, odd_y, a[1], a[2], a[1] @ a[1], b[1], b[2], b[1] @ b[1],
         both, both**2, np.tile(2.0 * rate_y[None, :], (m, 1)), np.tile(2.0 * rate_x[:, None], (1, m))]
    ).astype(np.float32)
    deep = (W + 1) * m
    tables = [
        halves(u_few),
        halves(np.swapaxes(u[:, :tall].reshape(PX, cx, tall), 1, 2)),
        halves(v),
        halves(v_few.T),
        halves(np.concatenate([t[:tall] for t in tu], 1).T),
        halves(np.concatenate(tv, 1)),
        halves(ends.reshape(64, m)),
        halves(corner),
    ]
    any_space = pl.BlockSpec(memory_space=pl.ANY)
    vmem = pl.BlockSpec(memory_space=pltpu.VMEM)
    dma = pltpu.SemaphoreType.DMA
    coeffs = pltpu.VMEM((W, m // 2, lanes), F32)
    thin = m // 2 + 16
    held = pl.pallas_call(
        functools.partial(kernel, dims, owners),
        out_shape=(
            pltpu.VMEM((L, cx, cy), F32),
            pltpu.VMEM((L, m // 2, lanes), F32),
        ),
        in_specs=[any_space] * 13,
        out_specs=(any_space, any_space),
        scratch_shapes=[
            pltpu.VMEM((L, cx, cy), F32),
            pltpu.VMEM((L, thin, lanes), F32),
            pltpu.VMEM((2, G, thin, lanes), F32),
            pltpu.VMEM((cx * L // 16, 128), F32),
            pltpu.VMEM((2, cx * L // 16, 128), F32),
            pltpu.VMEM((L, cx + 16, cy + 128), F32),
            pltpu.VMEM((L, cx, cy), F32),
            pltpu.VMEM((L, cx, cy), F32),
            pltpu.VMEM((L, m // 2 + 8, lanes), F32),
            pltpu.VMEM((2, cx, tall), BF16),
            pltpu.VMEM((2, tall, cy), BF16),
            pltpu.VMEM((2, m // 2 + 8, lanes), F32),
            pltpu.VMEM((2, m // 2, lanes), F32),
            pltpu.VMEM((W, m, m), F32),
            coeffs,
            coeffs,
            pltpu.VMEM((8, 128), F32),
            pltpu.VMEM((8, 128), F32),
            pltpu.VMEM((5, m, m), F32),
            pltpu.VMEM((2, tall, cx), BF16),
            pltpu.VMEM((2, cy, lanes), BF16),
            pltpu.VMEM((2, deep, tall), BF16),
            pltpu.VMEM((2, lanes, deep), BF16),
            pltpu.VMEM((2, 64, m), BF16),
            pltpu.VMEM((2, m, lanes), BF16),
            pltpu.VMEM((14, m, m), F32),
            pltpu.SMEM(relax_rates.shape, F32),
            pltpu.SMEM(nest_offsets.shape[::-1], jnp.int32),
            dma((L + 12,)),
            dma((L,)),
            dma((2, G)),
            dma((4,)),
            dma((4,)),
            dma((2,)),
            dma((2,)),
            dma((L,)),
            dma((2, G)),
            dma((L,)),
            dma((2, G)),
            dma((L,)),
        ],
        compiler_params=pltpu.CompilerParams(collective_id=0, has_side_effects=True),
    )(initial_state, drive_modes, relax_rates, nest_offsets.T,
      *(jnp.asarray(t) for t in tables), jnp.asarray(small))
    return pl.pallas_call(
        store,
        out_shape=[
            jax.ShapeDtypeStruct((1, L, cx, cy), F32),
            jax.ShapeDtypeStruct((1, L, m, m), F32),
        ],
        in_specs=[any_space, vmem],
        out_specs=[any_space] * 2,
        scratch_shapes=[pltpu.VMEM((L, m, m), F32), dma((2,))],
    )(*(pltpu.with_memory_space_constraint(x, pltpu.VMEM) for x in held))


def solution(mesh):
    nests, PY, PX = (mesh.shape[n] for n in ("nest", "py", "px"))
    spec = P("nest", None, "px", "py")

    def local(initial_state, drive_modes, relax_rates, nest_offsets):
        _, L, cx, cy = initial_state.shape
        W, _, m, _ = drive_modes.shape
        places = sorted(
            range(PY * PX),
            key=lambda g: (abs(2 * (g // PY) - PX + 1) + abs(2 * (g % PY) - PY + 1), g),
        )
        dims = (nests, PY, PX, L, cx, cy, m, W)
        return body(dims, tuple(places[:L]), initial_state, drive_modes, relax_rates, nest_offsets)

    return jax.shard_map(
        local,
        mesh=mesh,
        in_specs=(spec, P(), P("nest", None), P()),
        out_specs=(spec, P("nest", None, None, None)),
        check_vma=False,
    )
```

time: 24.4 us -> 21.9 us (0.90)
  local copies, waits for them, and re-layouts: 1.31 us -> 0 us
  Pallas kernels: 22.1 us -> 21.1 us
    pallas_call x1, Pallas kernels: 22.1 us -> 20.3 us  [body(): pl.pallas_call(functools.partial(kernel, dims, owners), out_shape=(pltpu....]
    unnamed x2 -> x0, local copies, waits for them, and re-layouts: 1.31 us -> none
    pallas_call x0 -> x1, Pallas kernels: none -> 0.76 us  [body(): pl.pallas_call(store, out_shape=[jax.ShapeDtypeStruct((1, L, cx, cy), F32...]
where the time goes in v4:
time: 21.9 us; the launch traced here: 21.7 us
  Pallas kernels  21.1 us (96%)
  between operations  0.64 us (3%)
    pallas_call x1, Pallas kernels, body(): pl.pallas_call(functools.partial(kernel, dims, owners), out_shape=(pltpu....  20.3 us
    pallas_call x1, Pallas kernels, body(): pl.pallas_call(store, out_shape=[jax.ShapeDtypeStruct((1, L, cx, cy), F32...  0.76 us

profile of v4, /device:TPU:3, one launch (start us, length us, event | category | flops | bytes accessed | tf_op | source)
XLA Modules:
  0.0 21.7 jit_solution(16025335938876337510)
XLA Ops:
  0.6 20.3 %shard_map.140 = (f32[4,64,128]{2,1,0:T(8,128)S(1)}, f32[4,32,128]{2,1,0:T(8,128)S(1)}) custom-call(f32[1,4,64,128]{3,2,1,0:T(8,128)} %field.1, f32[3,4,64,64]{3,2,1,0:T(8,128)} %drive.1, f32[1,4]{1,0:T(1,128)} %relax_hbm.1, s32[2,4]{1,0:T(2,128)} %bitcast.1, bf16[2,256,80]{2,1,0:T(8,128)(2,1)} %constant.18.clone.u_hbm, ...), custom_call_target="tpu_custom_call" | custom-call | tf_op jit(solution)/shard_map/pallas_call | solution.py:656
  20.9 0.8 %shard_map.141 = (f32[1,4,64,128]{3,2,1,0:T(8,128)}, f32[1,4,64,64]{3,2,1,0:T(8,128)}) custom-call(f32[4,64,128]{2,1,0:T(8,128)S(1)} %get-tuple-element.4.state, f32[4,32,128]{2,1,0:T(8,128)S(1)} %get-tuple-element.5.packed), custom_call_target="tpu_custom_call" | custom-call | tf_op jit(solution)/shard_map/pallas_call | solution.py:709

commit v5 on v4

--- a/solution.py
+++ b/solution.py
@@ -106,11 +106,11 @@
 def kernel(
     dims, owners,
     field, drive, relax_hbm, offs_hbm,
-    u_hbm, ut_hbm, v_hbm, vt_hbm, left_hbm, right_hbm, up_hbm, down_hbm, small_hbm,
+    u_hbm, ut_hbm, v_hbm, vt_hbm, left_hbm, right_hbm, up_hbm, small_hbm,
     out, modes,
-    fvm, pbuf, abuf, strip, near, wide, calm, state, fix, u_t, vt_t, zbuf, mail, start, par, cbuf, lead, glead, tx,
-    ut_t, v_t, left, right, up, down, small, relax, offs,
-    load_sem, a_send, a_recv, h_send, h_recv, c_sem, g_sem, out_sem, f_send, f_recv, m_send, m_recv,
+    fvm, pbuf, abuf, strip, near, wide, calm, state, fix, tally, u_t, vt_t, zbuf, mail, start, par, cbuf, lead, glead, tx,
+    ut_t, v_t, left, right, up, small, relax, offs,
+    load_sem, a_send, a_recv, h_send, h_recv, c_sem, g_sem, out_sem, b_send, f_recv, m_recv,
 ):
     nests, PY, PX, L, cx, cy, m, W = dims
     G, nx, ny = PY * PX, cx * PX, cy * PY
@@ -176,23 +176,22 @@
     chain_out = hop_copy(cbuf, par, c_sem.at[0], c_sem.at[1], 2)
     chain_in = hop_copy(cbuf, par, c_sem.at[0], c_sem.at[1], -2)
 
-    loads = [pltpu.make_async_copy(field.at[0, l], fvm.at[l], load_sem.at[l]) for l in range(L)]
-    for c in loads:
-        c.start()
+    load = pltpu.make_async_copy(field.at[0], fvm, load_sem.at[0])
+    load.start()
     rows_here = pl.ds(pl.multiple_of(px * cx, 8), cx)
     cols_here = pl.ds(pl.multiple_of(py * cy, 128), cy)
     pairs = [
         (v_hbm.at[:, cols_here], v_t), (ut_hbm.at[:, px], ut_t),
         (u_hbm.at[:, rows_here], u_t), (vt_hbm.at[:, :, cols_here], vt_t),
         (relax_hbm, relax), (offs_hbm, offs), (small_hbm, small),
-        (left_hbm, left), (right_hbm, right), (up_hbm, up), (down_hbm, down),
+        (left_hbm, left), (right_hbm, right), (up_hbm, up),
     ]
     tables = [
-        pltpu.make_async_copy(src, dst, load_sem.at[L + 1 + i]) for i, (src, dst) in enumerate(pairs)
+        pltpu.make_async_copy(src, dst, load_sem.at[2 + i]) for i, (src, dst) in enumerate(pairs)
     ]
     for c in tables[:4]:
         c.start()
-    get_drive = pltpu.make_async_copy(drive.at[:, level], start, load_sem.at[L])
+    get_drive = pltpu.make_async_copy(drive.at[:, level], start, load_sem.at[1])
 
     @pl.when(in_place)
     def _():
@@ -209,8 +208,7 @@
 
     tables[0].wait()
     tables[1].wait()
-    for c in loads:
-        c.wait()
+    load.wait()
     half = dot3(fvm[...].reshape(L * cx, cy), (v_t[0], v_t[1]))
     for l in range(L):
         pbuf[l] = pack_wide(dot3((ut_t[0], ut_t[1]), half[l * cx : (l + 1) * cx]), m)
@@ -253,7 +251,7 @@
 
     @pl.when(is_owner)
     def _():
-        abuf[1, me] = pbuf[level]
+        abuf[G + me] = pbuf[level]
         pl.semaphore_wait(barrier, beside + 2 * G - 1 + sum(jnp.where(c, 1, 0) for _, c in hops))
 
     @pl.when(jnp.logical_not(is_owner))
@@ -268,10 +266,15 @@
 
     def share(l):
         return remote(
-            pbuf.at[l], abuf.at[k % 2, me], a_send.at[l], a_recv.at[k % 2, me], owners[l], leader
+            pbuf.at[l], abuf.at[(k % 2) * G + me], a_send, a_recv, owners[l], leader
         )
 
-    keep_modes = pltpu.make_async_copy(mail.at[1], modes.at[level], m_recv.at[level])
+    def settled(ref, sem):
+        pltpu.make_async_copy(ref, ref, sem).wait()
+
+    part = jnp.where(level < L // 2, 0, 1)
+    keep_modes = pltpu.make_async_copy(mail.at[1], modes.at[level], m_recv)
+    keep_fix = pltpu.make_async_copy(zbuf.at[1], fix.at[level], f_recv.at[part])
 
     def beam(src, dst, i, device):
         return pltpu.make_async_remote_copy(
@@ -419,21 +422,15 @@
         tables[7].wait()
         tables[8].wait()
 
-        def arrive(g):
-            remote(pbuf.at[0], abuf.at[0, g], a_send.at[0], a_recv.at[0, g], g, k - 1).wait_recv()
-
-            @pl.when(g != me)
-            def _():
-                remote(pbuf.at[0], abuf.at[1, g], a_send.at[0], a_recv.at[1, g], g, k).wait_recv()
-        loop(G, arrive)
+        settled(abuf.at[pl.ds(0, 2 * G - 1)], a_recv)
 
         def project(i):
-            total = abuf[i, 0]
+            total = abuf[i * G]
             if G <= 16:
                 for g in range(1, G):
-                    total = total + abuf[i, g]
+                    total = total + abuf[i * G + g]
             else:
-                total = lax.fori_loop(1, G, lambda g, c: c + abuf[i, g], total)
+                total = lax.fori_loop(1, G, lambda g, c: c + abuf[i * G + g], total)
             both = dot3((left[0], left[1]), dot3(unpack_wide(total, m), (right[0], right[1])))
 
             def block(i, j):
@@ -464,25 +461,12 @@
             first([unpack(par[w]) for w in range(W)])
 
         d_lead, c_lead = nudge(before, [tx[i] for i in range(5)], lead_gain)
-        d_own, c_own = nudge(after, follow(c_lead, own_maps), gain)
-        for w in range(W):
-            cbuf[w] = pack(c_own[w])
-
-        @pl.when(k < nests - 2)
-        def _():
-            chain_out.start()
-
-        @pl.when(k < 2)
-        def _():
-            widen_patch()
-
         tables[9].wait()
-        tables[10].wait()
         def widen(x):
             return jnp.concatenate([x, jnp.zeros_like(x)], 1)
 
         def table(i):
-            return up[0, 16 * i : 16 * (i + 1)], up[1, 16 * i : 16 * (i + 1)]
+            return up[0, 16 * i : 16 * (i + 1), :m], up[1, 16 * i : 16 * (i + 1), :m]
 
         def correct(d):
             d1, d2, d3 = d
@@ -490,34 +474,60 @@
             main = d3 + small[10] * d2 + small[11] * d1
             rows = dot3(table(0), d2 + small[12] * d1) + dot3(table(1), e1)
             cols = dot3t(table(2), d2 + small[13] * d1) + dot3t(table(3), e1)
-            corner = dot3(dot3(table(0), e1), (down[0], down[1]))
+            corner = dot3(dot3(table(0), e1), (up[0, 64:], up[1, 64:]))
             return jnp.concatenate([pack(main), (widen(rows + cols) + corner)[:8]], 0)
 
-        zbuf[0] = correct(d_lead)
-        mail[0] = pack(c_lead[W - 1])
+        def mend(i, g):
+            return remote(
+                zbuf.at[i], fix.at[level], b_send, f_recv.at[part], g, k - 1 + i
+            )
+
+        def tell(i, g):
+            return remote(
+                mail.at[i], modes.at[level], b_send, m_recv, g, k - 1 + i
+            )
+
+        def give(i):
+            for copy in (mend, tell):
+                def one(j):
+                    g = jnp.where(2 * px < PX, G - 1 - j, j)
+                    if i == 0:
+                        copy(i, g).start()
+                    else:
+                        @pl.when(g != me)
+                        def _():
+                            copy(i, g).start()
+                loop(G, one)
+
+        def advance():
+            zbuf[0] = correct(d_lead)
+            mail[0] = pack(c_lead[W - 1])
+            give(0)
+
+        @pl.when(k >= nests - 2)
+        def _():
+            advance()
+
+        d_own, c_own = nudge(after, follow(c_lead, own_maps), gain)
+        for w in range(W):
+            cbuf[w] = pack(c_own[w])
+
+        @pl.when(k < nests - 2)
+        def _():
+            chain_out.start()
+
+        @pl.when(k < 2)
+        def _():
+            widen_patch()
+
+        @pl.when(k < nests - 2)
+        def _():
+            advance()
+
         zbuf[1] = correct(d_own)
         mail[1] = pack(c_own[W - 1])
-
-        def mend(i, g):
-            return remote(
-                zbuf.at[i], fix.at[level], f_send.at[i, g], f_recv.at[level], g, k - 1 + i
-            )
-
-        def tell(i, g):
-            return remote(
-                mail.at[i], modes.at[level], m_send.at[i, g], m_recv.at[level], g, k - 1 + i
-            )
-
-        for copy in (mend, tell):
-            for i in range(2):
-                def one(j):
-                    g = jnp.where(2 * px < PX, G - 1 - j, j)
-
-                    @pl.when(jnp.logical_or(i == 0, g != me))
-                    def _():
-                        copy(i, g).start()
-                loop(G, one)
-        fix[level] = zbuf[1]
+        give(1)
+        keep_fix.start()
         keep_modes.start()
         run_free()
 
@@ -529,45 +539,27 @@
     tables[2].wait()
     tables[3].wait()
 
-    puts = [pltpu.make_async_copy(state.at[l], out.at[l], out_sem.at[l]) for l in range(L)]
-
-    def finish(some):
-        for l in some:
-            @pl.when(jnp.logical_not(owns[l]))
-            def _():
-                remote(
-                    zbuf.at[0], fix.at[l], f_send.at[0, 0], f_recv.at[l], owners[l], leader
-                ).wait_recv()
+    puts = [pltpu.make_async_copy(state.at[l], out.at[l], out_sem) for l in range(L)]
+
+    def finish(i, some):
+        settled(fix.at[pl.ds(some[0], len(some))], f_recv.at[i])
         half = [dot3(unpack_fix(fix[l], m), (vt_t[0], vt_t[1])) for l in some]
         for l, x in zip(some, half):
             state[l] = calm[l] + dot3((u_t[0], u_t[1]), x)
             puts[l].start()
 
-    finish(range(L // 2))
-    finish(range(L // 2, L))
-    for l, o in enumerate(owners):
-        @pl.when(jnp.logical_not(owns[l]))
-        def _():
-            remote(
-                mail.at[0], modes.at[l], m_send.at[0, 0], m_recv.at[l], o, leader
-            ).wait_recv()
-            share(l).wait_send()
+    finish(0, range(L // 2))
+    finish(1, range(L // 2, L))
+    settled(modes, m_recv)
+
+    @pl.when(jnp.logical_not(is_owner))
+    def _():
+        settled(pbuf, a_send)
 
     @pl.when(is_owner)
     def _():
-        keep_modes.wait()
-
-        def drain(g):
-            for i in range(2):
-                @pl.when(jnp.logical_or(i == 0, g != me))
-                def _():
-                    remote(
-                        mail.at[i], modes.at[0], m_send.at[i, g], m_recv.at[0], g, k - 1 + i
-                    ).wait_send()
-                    remote(
-                        zbuf.at[i], fix.at[0], f_send.at[i, g], f_recv.at[0], g, k - 1 + i
-                    ).wait_send()
-        loop(G, drain)
+        settled(pbuf.at[pl.ds(0, L - 1)], a_send)
+        settled(tally, b_send)
 
         @pl.when(k < nests - 2)
         def _():
@@ -581,8 +573,7 @@
         @pl.when(sides[i][0])
         def _():
             halo[i].wait_send()
-    for c in puts:
-        c.wait()
+    settled(state, out_sem)
 
 
 def store(state, packed, state_out, modes_out, modes, sem):
@@ -645,8 +636,7 @@
         halves(v_few.T),
         halves(np.concatenate([t[:tall] for t in tu], 1).T),
         halves(np.concatenate(tv, 1)),
-        halves(ends.reshape(64, m)),
-        halves(corner),
+        halves(np.concatenate([np.pad(ends.reshape(64, m), ((0, 0), (0, m))), corner], 0)),
     ]
     any_space = pl.BlockSpec(memory_space=pl.ANY)
     vmem = pl.BlockSpec(memory_space=pltpu.VMEM)
@@ -659,18 +649,19 @@
             pltpu.VMEM((L, cx, cy), F32),
             pltpu.VMEM((L, m // 2, lanes), F32),
         ),
-        in_specs=[any_space] * 13,
+        in_specs=[any_space] * 12,
         out_specs=(any_space, any_space),
         scratch_shapes=[
             pltpu.VMEM((L, cx, cy), F32),
             pltpu.VMEM((L, thin, lanes), F32),
-            pltpu.VMEM((2, G, thin, lanes), F32),
+            pltpu.VMEM((2 * G, thin, lanes), F32),
             pltpu.VMEM((cx * L // 16, 128), F32),
             pltpu.VMEM((2, cx * L // 16, 128), F32),
             pltpu.VMEM((L, cx + 16, cy + 128), F32),
             pltpu.VMEM((L, cx, cy), F32),
             pltpu.VMEM((L, cx, cy), F32),
             pltpu.VMEM((L, m // 2 + 8, lanes), F32),
+            pltpu.VMEM((2 * G - 1, m + 8, lanes), F32),
             pltpu.VMEM((2, cx, tall), BF16),
             pltpu.VMEM((2, tall, cy), BF16),
             pltpu.VMEM((2, m // 2 + 8, lanes), F32),
@@ -685,23 +676,21 @@
             pltpu.VMEM((2, cy, lanes), BF16),
             pltpu.VMEM((2, deep, tall), BF16),
             pltpu.VMEM((2, lanes, deep), BF16),
-            pltpu.VMEM((2, 64, m), BF16),
-            pltpu.VMEM((2, m, lanes), BF16),
+            pltpu.VMEM((2, 64 + m, lanes), BF16),
             pltpu.VMEM((14, m, m), F32),
             pltpu.SMEM(relax_rates.shape, F32),
             pltpu.SMEM(nest_offsets.shape[::-1], jnp.int32),
-            dma((L + 12,)),
-            dma((L,)),
-            dma((2, G)),
+            dma((12,)),
+            dma,
+            dma,
             dma((4,)),
             dma((4,)),
             dma((2,)),
             dma((2,)),
-            dma((L,)),
-            dma((2, G)),
-            dma((L,)),
-            dma((2, G)),
-            dma((L,)),
+            dma,
+            dma,
+            dma((2,)),
+            dma,
         ],
         compiler_params=pltpu.CompilerParams(collective_id=0, has_side_effects=True),
     )(initial_state, drive_modes, relax_rates, nest_offsets.T,

time: 21.9 us -> 20.4 us (0.932)
  Pallas kernels: 21.1 us -> 19.6 us
    pallas_call x1, Pallas kernels: 20.3 us -> 18.8 us  [body(): pl.pallas_call(functools.partial(kernel, dims, owners), out_shape=(pltpu....]
where the time goes in v5:
time: 20.4 us; the launch traced here: 20.2 us
  Pallas kernels  19.6 us (96%)
  between operations  0.64 us (3%)
    pallas_call x1, Pallas kernels, body(): pl.pallas_call(functools.partial(kernel, dims, owners), out_shape=(pltpu....  18.8 us
    pallas_call x1, Pallas kernels, body(): pl.pallas_call(store, out_shape=[jax.ShapeDtypeStruct((1, L, cx, cy), F32...  0.76 us

profile of v5, /device:TPU:3, one launch (start us, length us, event | category | flops | bytes accessed | tf_op | source)
XLA Modules:
  0.0 20.2 jit_solution(14384036341124805785)
XLA Ops:
  0.6 18.8 %shard_map.131 = (f32[4,64,128]{2,1,0:T(8,128)S(1)}, f32[4,32,128]{2,1,0:T(8,128)S(1)}) custom-call(f32[1,4,64,128]{3,2,1,0:T(8,128)} %field.1, f32[3,4,64,64]{3,2,1,0:T(8,128)} %drive.1, f32[1,4]{1,0:T(1,128)} %relax_hbm.1, s32[2,4]{1,0:T(2,128)} %bitcast.1, bf16[2,256,80]{2,1,0:T(8,128)(2,1)} %constant.16.clone.u_hbm, ...), custom_call_target="tpu_custom_call" | custom-call | tf_op jit(solution)/shard_map/pallas_call | solution.py:646
  19.5 0.8 %shard_map.132 = (f32[1,4,64,128]{3,2,1,0:T(8,128)}, f32[1,4,64,64]{3,2,1,0:T(8,128)}) custom-call(f32[4,64,128]{2,1,0:T(8,128)S(1)} %get-tuple-element.4.state, f32[4,32,128]{2,1,0:T(8,128)S(1)} %get-tuple-element.5.packed), custom_call_target="tpu_custom_call" | custom-call | tf_op jit(solution)/shard_map/pallas_call | solution.py:698

commit v6 on v5

--- a/solution.py
+++ b/solution.py
@@ -137,45 +137,6 @@
         (py > 0, (k, py - 1, px)), (py < PY - 1, (k, py + 1, px)),
     ]
     beside = sum(jnp.where(c, 1, 0) for c, _ in sides)
-    barrier = pltpu.get_barrier_semaphore()
-    for l, o in enumerate(owners):
-        @pl.when(jnp.logical_not(owns[l]))
-        def _():
-            pl.semaphore_signal(barrier, inc=1, device_id=at(o, leader), device_id_type=MESH)
-
-    for cond, device in sides:
-        @pl.when(cond)
-        def _():
-            pl.semaphore_signal(barrier, inc=1, device_id=device, device_id_type=MESH)
-
-    @pl.when(is_owner)
-    def _():
-        def greet(g):
-            pl.semaphore_signal(barrier, inc=1, device_id=at(g, k - 1), device_id_type=MESH)
-
-            @pl.when(plain(g))
-            def _():
-                pl.semaphore_signal(barrier, inc=1, device_id=at(g, k), device_id_type=MESH)
-        loop(G, greet)
-
-        for hop, cond in hops:
-            @pl.when(cond)
-            def _():
-                pl.semaphore_signal(
-                    barrier, inc=1, device_id=(k + hop, py, px), device_id_type=MESH
-                )
-
-    def hop_copy(src, dst, send_sem, recv_sem, hop):
-        return pltpu.make_async_remote_copy(
-            src_ref=src, dst_ref=dst, send_sem=send_sem, recv_sem=recv_sem,
-            device_id=(k + hop, py, px), device_id_type=MESH,
-        )
-
-    gain_out = hop_copy(lead, glead, g_sem.at[0], g_sem.at[1], 1)
-    gain_in = hop_copy(lead, glead, g_sem.at[0], g_sem.at[1], -1)
-    chain_out = hop_copy(cbuf, par, c_sem.at[0], c_sem.at[1], 2)
-    chain_in = hop_copy(cbuf, par, c_sem.at[0], c_sem.at[1], -2)
-
     load = pltpu.make_async_copy(field.at[0], fvm, load_sem.at[0])
     load.start()
     rows_here = pl.ds(pl.multiple_of(px * cx, 8), cx)
@@ -191,6 +152,45 @@
     ]
     for c in tables[:4]:
         c.start()
+    barrier = pltpu.get_barrier_semaphore()
+    for l, o in enumerate(owners):
+        @pl.when(jnp.logical_not(owns[l]))
+        def _():
+            pl.semaphore_signal(barrier, inc=1, device_id=at(o, leader), device_id_type=MESH)
+
+    for cond, device in sides:
+        @pl.when(cond)
+        def _():
+            pl.semaphore_signal(barrier, inc=1, device_id=device, device_id_type=MESH)
+
+    @pl.when(is_owner)
+    def _():
+        def greet(g):
+            pl.semaphore_signal(barrier, inc=1, device_id=at(g, k - 1), device_id_type=MESH)
+
+            @pl.when(plain(g))
+            def _():
+                pl.semaphore_signal(barrier, inc=1, device_id=at(g, k), device_id_type=MESH)
+        loop(G, greet)
+
+        for hop, cond in hops:
+            @pl.when(cond)
+            def _():
+                pl.semaphore_signal(
+                    barrier, inc=1, device_id=(k + hop, py, px), device_id_type=MESH
+                )
+
+    def hop_copy(src, dst, send_sem, recv_sem, hop):
+        return pltpu.make_async_remote_copy(
+            src_ref=src, dst_ref=dst, send_sem=send_sem, recv_sem=recv_sem,
+            device_id=(k + hop, py, px), device_id_type=MESH,
+        )
+
+    gain_out = hop_copy(lead, glead, g_sem.at[0], g_sem.at[1], 1)
+    gain_in = hop_copy(lead, glead, g_sem.at[0], g_sem.at[1], -1)
+    chain_out = hop_copy(cbuf, par, c_sem.at[0], c_sem.at[1], 2)
+    chain_in = hop_copy(cbuf, par, c_sem.at[0], c_sem.at[1], -2)
+
     get_drive = pltpu.make_async_copy(drive.at[:, level], start, load_sem.at[1])
 
     @pl.when(in_place)
@@ -212,6 +212,69 @@
     half = dot3(fvm[...].reshape(L * cx, cy), (v_t[0], v_t[1]))
     for l in range(L):
         pbuf[l] = pack_wide(dot3((ut_t[0], ut_t[1]), half[l * cx : (l + 1) * cx]), m)
+
+    @pl.when(is_owner)
+    def _():
+        abuf[G + me] = pbuf[level]
+        pl.semaphore_wait(barrier, beside + 2 * G - 1 + sum(jnp.where(c, 1, 0) for _, c in hops))
+
+    @pl.when(jnp.logical_not(is_owner))
+    def _():
+        pl.semaphore_wait(barrier, beside + L)
+
+    def remote(src, dst, send_sem, recv_sem, g, nest):
+        return pltpu.make_async_remote_copy(
+            src_ref=src, dst_ref=dst, send_sem=send_sem, recv_sem=recv_sem,
+            device_id=at(g, nest), device_id_type=MESH,
+        )
+
+    def share(l):
+        return remote(
+            pbuf.at[l], abuf.at[(k % 2) * G + me], a_send, a_recv, owners[l], leader
+        )
+
+    def settled(ref, sem):
+        pltpu.make_async_copy(ref, ref, sem).wait()
+
+    part = jnp.where(level < L // 2, 0, 1)
+    keep_modes = pltpu.make_async_copy(mail.at[1], modes.at[level], m_recv)
+    keep_fix = pltpu.make_async_copy(zbuf.at[1], fix.at[level], f_recv.at[part])
+
+    def beam(src, dst, i, device):
+        return pltpu.make_async_remote_copy(
+            src_ref=src, dst_ref=dst, send_sem=h_send.at[i], recv_sem=h_recv.at[i],
+            device_id=device, device_id_type=MESH,
+        )
+
+    top, bottom = pl.ds(0, 8), pl.ds(cx + 8, 8)
+    first_rows, last_rows = pl.ds(8, 8), pl.ds(cx, 8)
+    halo = [
+        beam(wide.at[:, first_rows], wide.at[:, bottom], 0, sides[0][1]),
+        beam(wide.at[:, last_rows], wide.at[:, top], 1, sides[1][1]),
+        beam(strip, near.at[1], 2, sides[2][1]),
+        beam(strip, near.at[0], 3, sides[3][1]),
+    ]
+
+    def start_halo(i):
+        @pl.when(sides[i][0])
+        def _():
+            halo[i].start()
+
+    def land_halo(i):
+        @pl.when(sides[i ^ 1][0])
+        def _():
+            halo[i].wait_recv()
+
+    for l, o in enumerate(owners):
+        @pl.when(jnp.logical_not(owns[l]))
+        def _():
+            share(l).start()
+
+    @pl.when(is_spare)
+    def _():
+        tables[4].wait()
+        lead[...] = jnp.full(lead.shape, relax[0, level], F32)
+        gain_out.start()
 
     lane = lax.broadcasted_iota(jnp.int32, (cx, 128), 1)
     edge = jnp.zeros((cx, 128), F32)
@@ -249,69 +312,6 @@
     def _():
         near[1] = jnp.zeros(near.shape[1:], F32)
 
-    @pl.when(is_owner)
-    def _():
-        abuf[G + me] = pbuf[level]
-        pl.semaphore_wait(barrier, beside + 2 * G - 1 + sum(jnp.where(c, 1, 0) for _, c in hops))
-
-    @pl.when(jnp.logical_not(is_owner))
-    def _():
-        pl.semaphore_wait(barrier, beside + L)
-
-    def remote(src, dst, send_sem, recv_sem, g, nest):
-        return pltpu.make_async_remote_copy(
-            src_ref=src, dst_ref=dst, send_sem=send_sem, recv_sem=recv_sem,
-            device_id=at(g, nest), device_id_type=MESH,
-        )
-
-    def share(l):
-        return remote(
-            pbuf.at[l], abuf.at[(k % 2) * G + me], a_send, a_recv, owners[l], leader
-        )
-
-    def settled(ref, sem):
-        pltpu.make_async_copy(ref, ref, sem).wait()
-
-    part = jnp.where(level < L // 2, 0, 1)
-    keep_modes = pltpu.make_async_copy(mail.at[1], modes.at[level], m_recv)
-    keep_fix = pltpu.make_async_copy(zbuf.at[1], fix.at[level], f_recv.at[part])
-
-    def beam(src, dst, i, device):
-        return pltpu.make_async_remote_copy(
-            src_ref=src, dst_ref=dst, send_sem=h_send.at[i], recv_sem=h_recv.at[i],
-            device_id=device, device_id_type=MESH,
-        )
-
-    top, bottom = pl.ds(0, 8), pl.ds(cx + 8, 8)
-    first_rows, last_rows = pl.ds(8, 8), pl.ds(cx, 8)
-    halo = [
-        beam(wide.at[:, first_rows], wide.at[:, bottom], 0, sides[0][1]),
-        beam(wide.at[:, last_rows], wide.at[:, top], 1, sides[1][1]),
-        beam(strip, near.at[1], 2, sides[2][1]),
-        beam(strip, near.at[0], 3, sides[3][1]),
-    ]
-
-    def start_halo(i):
-        @pl.when(sides[i][0])
-        def _():
-            halo[i].start()
-
-    def land_halo(i):
-        @pl.when(sides[i ^ 1][0])
-        def _():
-            halo[i].wait_recv()
-
-    for l, o in enumerate(owners):
-        @pl.when(jnp.logical_not(owns[l]))
-        def _():
-            share(l).start()
-
-    @pl.when(is_spare)
-    def _():
-        tables[4].wait()
-        lead[...] = jnp.full(lead.shape, relax[0, level], F32)
-        gain_out.start()
-
     start_halo(2)
     start_halo(3)
 
@@ -431,14 +431,29 @@
                     total = total + abuf[i * G + g]
             else:
                 total = lax.fori_loop(1, G, lambda g, c: c + abuf[i * G + g], total)
-            both = dot3((left[0], left[1]), dot3(unpack_wide(total, m), (right[0], right[1])))
-
-            def block(i, j):
-                return both[i * m : (i + 1) * m, j * m : (j + 1) * m]
+            main = unpack(total[: m // 2])
+            edge = total[m // 2 : m // 2 + 8]
+            low = jnp.concatenate([total[m // 2 + 8 :, :m], jnp.zeros((m - 8, m), F32)], 0).T
+            low = split(low[:, :16])
+            none = jnp.zeros_like(edge)
+            row0 = jnp.concatenate([edge[:, :m], none[:, :m]], 0)
+            edge = split(jnp.concatenate([edge, none], 0))
+
+            def table(start, size):
+                return right[0, start : start + size], right[1, start : start + size]
+
+            row1, row2 = (dot3(edge, table(2 * m * j, 2 * m)) for j in range(2))
+            q1, q2, q3 = (dot3(low, table(4 * m + 16 * j, 16)) for j in range(3))
+
+            def rows(*parts):
+                size = 16 * len(parts)
+                return dot3((left[0, :, :size], left[1, :, :size]), jnp.concatenate(parts, 0))
 
             return [
-                sum(float(math.comb(w, i)) * block(i, w - i) for i in range(w + 1))
-                for w in (1, 2, 3)
+                small[10] * main + (rows(row0) + q1),
+                small[11] * main + (rows(2.0 * row1, row0) + small[13] * q1 + q2),
+                small[14] * main
+                + (rows(3.0 * row2, 3.0 * row1, row0) + small[15] * q1 + 1.5 * small[13] * q2 + q3),
             ]
 
         def settle(s, rate):
@@ -487,22 +502,22 @@
                 mail.at[i], modes.at[level], b_send, m_recv, g, k - 1 + i
             )
 
-        def give(i):
-            for copy in (mend, tell):
-                def one(j):
-                    g = jnp.where(2 * px < PX, G - 1 - j, j)
-                    if i == 0:
+        def give(copy, i):
+            def one(j):
+                g = jnp.where(2 * px < PX, G - 1 - j, j)
+                if i == 0:
+                    copy(i, g).start()
+                else:
+                    @pl.when(g != me)
+                    def _():
                         copy(i, g).start()
-                    else:
-                        @pl.when(g != me)
-                        def _():
-                            copy(i, g).start()
-                loop(G, one)
+            loop(G, one)
 
         def advance():
+            mail[0] = pack(c_lead[W - 1])
+            give(tell, 0)
             zbuf[0] = correct(d_lead)
-            mail[0] = pack(c_lead[W - 1])
-            give(0)
+            give(mend, 0)
 
         @pl.when(k >= nests - 2)
         def _():
@@ -525,8 +540,9 @@
             advance()
 
         zbuf[1] = correct(d_own)
+        give(mend, 1)
         mail[1] = pack(c_own[W - 1])
-        give(1)
+        give(tell, 1)
         keep_fix.start()
         keep_modes.start()
         run_free()
@@ -539,17 +555,18 @@
     tables[2].wait()
     tables[3].wait()
 
-    puts = [pltpu.make_async_copy(state.at[l], out.at[l], out_sem) for l in range(L)]
-
-    def finish(i, some):
-        settled(fix.at[pl.ds(some[0], len(some))], f_recv.at[i])
-        half = [dot3(unpack_fix(fix[l], m), (vt_t[0], vt_t[1])) for l in some]
-        for l, x in zip(some, half):
-            state[l] = calm[l] + dot3((u_t[0], u_t[1]), x)
-            puts[l].start()
-
-    finish(0, range(L // 2))
-    finish(1, range(L // 2, L))
+    most = L // 2
+    far = jnp.where(2 * px < PX, 0, 1)
+    for i in range(2):
+        turn = (i + far) % 2
+        first = turn * most
+        some = pl.ds(first, most)
+        settled(fix.at[some], f_recv.at[turn])
+        half = [dot3(unpack_fix(fix[first + j], m), (vt_t[0], vt_t[1])) for j in range(most)]
+        done = [calm[first + j] + dot3((u_t[0], u_t[1]), half[j]) for j in range(most)]
+        for j in range(most):
+            state[first + j] = done[j]
+        pltpu.make_async_copy(state.at[some], out.at[some], out_sem).start()
     settled(modes, m_recv)
 
     @pl.when(jnp.logical_not(is_owner))
@@ -605,7 +622,7 @@
 def body(dims, owners, initial_state, drive_modes, relax_rates, nest_offsets):
     nests, PY, PX, L, cx, cy, m, W = dims
     G, nx, ny = PY * PX, cx * PX, cy * PY
-    assert nests % 2 == 0 and W == 3
+    assert nests % 2 == 0 and L % 2 == 0 and W == 3
     tall, lanes = m + 16, 2 * m
     rp, u, tu, rate_x = wide_tables(nx, m, W)
     cp, v, tv, rate_y = wide_tables(ny, m, W)
@@ -626,7 +643,8 @@
     even_y, odd_y = ((cp[0].T @ basis(ny, m, RATIO, f)).T for f in (np.cos, np.sin))
     small = np.stack(
         [even_x, odd_x, even_y, odd_y, a[1], a[2], a[1] @ a[1], b[1], b[2], b[1] @ b[1],
-         both, both**2, np.tile(2.0 * rate_y[None, :], (m, 1)), np.tile(2.0 * rate_x[:, None], (1, m))]
+         both, both**2, np.tile(2.0 * rate_y[None, :], (m, 1)), np.tile(2.0 * rate_x[:, None], (1, m)),
+         both**3, np.tile(3.0 * rate_x[:, None] ** 2, (1, m))]
     ).astype(np.float32)
     deep = (W + 1) * m
     tables = [
@@ -634,8 +652,8 @@
         halves(np.swapaxes(u[:, :tall].reshape(PX, cx, tall), 1, 2)),
         halves(v),
         halves(v_few.T),
-        halves(np.concatenate([t[:tall] for t in tu], 1).T),
-        halves(np.concatenate(tv, 1)),
+        halves(np.concatenate([t[m:tall].T for t in tu[1:]], 1)),
+        halves(np.concatenate(tv[1:3] + [t[m : m + 16] for t in tv[1:]], 0)),
         halves(np.concatenate([np.pad(ends.reshape(64, m), ((0, 0), (0, m))), corner], 0)),
     ]
     any_space = pl.BlockSpec(memory_space=pl.ANY)
@@ -674,10 +692,10 @@
             pltpu.VMEM((5, m, m), F32),
             pltpu.VMEM((2, tall, cx), BF16),
             pltpu.VMEM((2, cy, lanes), BF16),
-            pltpu.VMEM((2, deep, tall), BF16),
-            pltpu.VMEM((2, lanes, deep), BF16),
+            pltpu.VMEM((2, m, 16 * W), BF16),
+            pltpu.VMEM((2, 4 * m + 16 * W, m), BF16),
             pltpu.VMEM((2, 64 + m, lanes), BF16),
-            pltpu.VMEM((14, m, m), F32),
+            pltpu.VMEM((16, m, m), F32),
             pltpu.SMEM(relax_rates.shape, F32),
             pltpu.SMEM(nest_offsets.shape[::-1], jnp.int32),
             dma((12,)),

time: 20.4 us -> 19 us (0.931)
  Pallas kernels: 19.6 us -> 18.2 us
    pallas_call x1, Pallas kernels: 18.8 us -> 17.5 us  [body(): pl.pallas_call(functools.partial(kernel, dims, owners), out_shape=(pltpu....]
where the time goes in v6:
time: 19 us; the launch traced here: 18.9 us
  Pallas kernels  18.2 us (96%)
  between operations  0.64 us (3%)
    pallas_call x1, Pallas kernels, body(): pl.pallas_call(functools.partial(kernel, dims, owners), out_shape=(pltpu....  17.5 us
    pallas_call x1, Pallas kernels, body(): pl.pallas_call(store, out_shape=[jax.ShapeDtypeStruct((1, L, cx, cy), F32...  0.76 us

profile of v6, /device:TPU:3, one launch (start us, length us, event | category | flops | bytes accessed | tf_op | source)
XLA Modules:
  0.0 18.9 jit_solution(6673390089295584568)
XLA Ops:
  0.6 17.5 %shard_map.131 = (f32[4,64,128]{2,1,0:T(8,128)S(1)}, f32[4,32,128]{2,1,0:T(8,128)S(1)}) custom-call(f32[1,4,64,128]{3,2,1,0:T(8,128)} %field.1, f32[3,4,64,64]{3,2,1,0:T(8,128)} %drive.1, f32[1,4]{1,0:T(1,128)} %relax_hbm.1, s32[2,4]{1,0:T(2,128)} %bitcast.1, bf16[2,256,80]{2,1,0:T(8,128)(2,1)} %constant.16.clone.u_hbm, ...), custom_call_target="tpu_custom_call" | custom-call | tf_op jit(solution)/shard_map/pallas_call | solution.py:664
  18.1 0.8 %shard_map.132 = (f32[1,4,64,128]{3,2,1,0:T(8,128)}, f32[1,4,64,64]{3,2,1,0:T(8,128)}) custom-call(f32[4,64,128]{2,1,0:T(8,128)S(1)} %get-tuple-element.4.state, f32[4,32,128]{2,1,0:T(8,128)S(1)} %get-tuple-element.5.packed), custom_call_target="tpu_custom_call" | custom-call | tf_op jit(solution)/shard_map/pallas_call | solution.py:716

commit v7 on v6

--- a/solution.py
+++ b/solution.py
@@ -63,6 +63,21 @@
         return lax.dot_general(x, y, (((1,), (1,)), ((), ())), preferred_element_type=F32)
 
     return nt(a[0], b[0]) + (nt(a[0], b[1]) + nt(a[1], b[0]))
+
+
+def tri(a):
+    return jnp.concatenate([a[0], a[0], a[1]], 1)
+
+
+def dotk(a, b):
+    b = b if isinstance(b, tuple) else split(b)
+    return mm(a, jnp.concatenate([b[0], b[1], b[0]], 0))
+
+
+def stack(*parts):
+    if isinstance(parts[0], tuple):
+        return tuple(jnp.concatenate(p, 0) for p in zip(*parts))
+    return jnp.concatenate(parts, 0)
 
 
 def pack(x):
@@ -137,12 +152,24 @@
         (py > 0, (k, py - 1, px)), (py < PY - 1, (k, py + 1, px)),
     ]
     beside = sum(jnp.where(c, 1, 0) for c, _ in sides)
+    barrier = pltpu.get_barrier_semaphore()
+
+    @pl.when(is_owner)
+    def _():
+        def greet(g):
+            pl.semaphore_signal(barrier, inc=1, device_id=at(g, k - 1), device_id_type=MESH)
+
+            @pl.when(plain(g))
+            def _():
+                pl.semaphore_signal(barrier, inc=1, device_id=at(g, k), device_id_type=MESH)
+        loop(G, greet)
+
     load = pltpu.make_async_copy(field.at[0], fvm, load_sem.at[0])
     load.start()
     rows_here = pl.ds(pl.multiple_of(px * cx, 8), cx)
     cols_here = pl.ds(pl.multiple_of(py * cy, 128), cy)
     pairs = [
-        (v_hbm.at[:, cols_here], v_t), (ut_hbm.at[:, px], ut_t),
+        (v_hbm.at[:, cols_here], v_t), (ut_hbm.at[px], ut_t),
         (u_hbm.at[:, rows_here], u_t), (vt_hbm.at[:, :, cols_here], vt_t),
         (relax_hbm, relax), (offs_hbm, offs), (small_hbm, small),
         (left_hbm, left), (right_hbm, right), (up_hbm, up),
@@ -152,7 +179,6 @@
     ]
     for c in tables[:4]:
         c.start()
-    barrier = pltpu.get_barrier_semaphore()
     for l, o in enumerate(owners):
         @pl.when(jnp.logical_not(owns[l]))
         def _():
@@ -165,14 +191,6 @@
 
     @pl.when(is_owner)
     def _():
-        def greet(g):
-            pl.semaphore_signal(barrier, inc=1, device_id=at(g, k - 1), device_id_type=MESH)
-
-            @pl.when(plain(g))
-            def _():
-                pl.semaphore_signal(barrier, inc=1, device_id=at(g, k), device_id_type=MESH)
-        loop(G, greet)
-
         for hop, cond in hops:
             @pl.when(cond)
             def _():
@@ -211,7 +229,7 @@
     load.wait()
     half = dot3(fvm[...].reshape(L * cx, cy), (v_t[0], v_t[1]))
     for l in range(L):
-        pbuf[l] = pack_wide(dot3((ut_t[0], ut_t[1]), half[l * cx : (l + 1) * cx]), m)
+        pbuf[l] = pack_wide(dotk(ut_t[...], half[l * cx : (l + 1) * cx]), m)
 
     @pl.when(is_owner)
     def _():
@@ -383,21 +401,25 @@
             a2, b2 = curved(rate)
             f0, g0 = flat(kk)
             f1, f2 = split(dot3(a1, f0)), split(dot3(a2, f0))
+            f01 = tuple(jnp.concatenate(p, 1) for p in zip(f0, f1))
             g1, g2 = split(dot3(g0, b1)), split(dot3(g0, b2))
-            return f0, f1, f2, g0, g1, g2, 2.0 * (1.0 - rate)
+            return tri(f0), tri(stack(f0, f1, f2)), tri(f01), g0, g1, g2, 2.0 * (1.0 - rate)
 
         def follow(cs, ms):
-            f0, f1, f2, g0, g1, g2, rest = ms
+            f0, f012, f01, g0, g1, g2, rest = ms
             c1, c2, c3 = (split(c) for c in cs)
-            y10, y20, y30 = dot3(c1, g0), dot3(c2, g0), dot3(c3, g0)
-            y11, y21, y12 = dot3(c1, g1), dot3(c2, g1), dot3(c1, g2)
-            y10s = split(y10)
+            y0 = dot3(stack(c1, c2, c3), g0)
+            y1 = dot3(stack(c1, c2), g1)
+            y12 = dot3(c1, g2)
+            y10, y20, y30 = y0[:m], y0[m : 2 * m], y0[2 * m :]
+            y11, y21 = y1[:m], y1[m:]
+            z = dotk(f012, y10)
             return (
-                dot3(f0, y10s),
-                dot3(f0, y20),
-                dot3(f0, y30),
-                dot3(f1, y10s) + dot3(f0, y11),
-                dot3(f0, y21 + y12) + dot3(f1, y20 + rest * y11) + dot3(f2, y10s),
+                z[:m],
+                dotk(f0, y20),
+                dotk(f0, y30),
+                z[m : 2 * m] + dotk(f0, y11),
+                z[2 * m :] + dotk(f01, stack(y21 + y12, y20 + rest * y11)),
             )
 
         def nudge(own, moved, rate):
@@ -410,6 +432,12 @@
         lead_gain = glead[0:1, 0:m]
         lead_maps = maps(k - 1, lead_gain)
 
+        def both_sides(rate):
+            a2, b2 = curved(rate)
+            return tri(a1), tri(stack(a1, a2)), b2
+
+        sides_lead, sides_own = both_sides(lead_gain), both_sides(gain)
+
         def first(cs):
             for i, x in enumerate(follow(cs, lead_maps)):
                 tx[i] = x
@@ -422,52 +450,62 @@
         tables[7].wait()
         tables[8].wait()
 
+        grown = [tri((left[0, :, : 16 * i], left[1, :, : 16 * i])) for i in (1, 2, 3)]
+        tables[9].wait()
+        ends = [tri((up[0, 16 * i : 16 * i + 16, :m], up[1, 16 * i : 16 * i + 16, :m])) for i in (0, 1)]
         settled(abuf.at[pl.ds(0, 2 * G - 1)], a_recv)
 
-        def project(i):
+        def gathered(i):
             total = abuf[i * G]
             if G <= 16:
                 for g in range(1, G):
                     total = total + abuf[i * G + g]
             else:
                 total = lax.fori_loop(1, G, lambda g, c: c + abuf[i * G + g], total)
-            main = unpack(total[: m // 2])
-            edge = total[m // 2 : m // 2 + 8]
-            low = jnp.concatenate([total[m // 2 + 8 :, :m], jnp.zeros((m - 8, m), F32)], 0).T
-            low = split(low[:, :16])
-            none = jnp.zeros_like(edge)
-            row0 = jnp.concatenate([edge[:, :m], none[:, :m]], 0)
-            edge = split(jnp.concatenate([edge, none], 0))
-
-            def table(start, size):
-                return right[0, start : start + size], right[1, start : start + size]
-
-            row1, row2 = (dot3(edge, table(2 * m * j, 2 * m)) for j in range(2))
-            q1, q2, q3 = (dot3(low, table(4 * m + 16 * j, 16)) for j in range(3))
-
-            def rows(*parts):
-                size = 16 * len(parts)
-                return dot3((left[0, :, :size], left[1, :, :size]), jnp.concatenate(parts, 0))
-
+            return total
+
+        def table(start, size):
+            return right[0, start : start + size], right[1, start : start + size]
+
+        def rows(*parts):
+            return dotk(grown[len(parts) - 1], jnp.concatenate(parts, 0))
+
+        totals = [gathered(i) for i in range(2)]
+        lows, edges = [], []
+        for t in totals:
+            low = t[m // 2 + 8 :, :m]
+            lows.append(jnp.concatenate([low, jnp.zeros((m - 8, m), F32)], 0).T[:, :16])
+            edges.append(t[m // 2 : m // 2 + 8])
+        lows, edges_s = split(stack(*lows)), split(stack(*edges))
+        row1, row2 = (dot3(edges_s, table(2 * m * j, 2 * m)) for j in range(2))
+        q1, q2, q3 = (dot3(lows, table(4 * m + 16 * j, 16)) for j in range(3))
+
+        def project(i):
+            main = unpack(totals[i][: m // 2])
+            none = jnp.zeros((8, m), F32)
+            r0 = stack(edges[i][:, :m], none)
+            r1, r2 = (stack(r[8 * i : 8 * i + 8], none) for r in (row1, row2))
+            p1, p2, p3 = (q[i * m : (i + 1) * m] for q in (q1, q2, q3))
             return [
-                small[10] * main + (rows(row0) + q1),
-                small[11] * main + (rows(2.0 * row1, row0) + small[13] * q1 + q2),
+                small[10] * main + (rows(r0) + p1),
+                small[11] * main + (rows(2.0 * r1, r0) + small[13] * p1 + p2),
                 small[14] * main
-                + (rows(3.0 * row2, 3.0 * row1, row0) + small[15] * q1 + 1.5 * small[13] * q2 + q3),
+                + (rows(3.0 * r2, 3.0 * r1, r0) + small[15] * p1 + 1.5 * small[13] * p2 + p3),
             ]
 
-        def settle(s, rate):
+        def settle(s, rate, sides):
             s1, s2, s3 = s
-            a2, b2 = curved(rate)
+            a1, a12, b2 = sides
             s1s, s2s = split(s1), split(s2)
-            z11 = dot3(s1s, b1)
-            x2 = dot3(a1, s1s) + z11
-            x3 = dot3(s2s, b1) + dot3(s1s, b2) + dot3(a2, s1s)
-            x3 = x3 + dot3(a1, s2 + 2.0 * (1.0 - rate) * z11)
+            by_b = dot3(stack(s1s, s2s), b1)
+            by_a = dotk(a12, s1s)
+            x2 = by_a[:m] + by_b[:m]
+            x3 = by_b[m:] + dot3(s1s, b2) + by_a[m:]
+            x3 = x3 + dotk(a1, s2 + 2.0 * (1.0 - rate) * by_b[:m])
             return s1, s2 - rate * x2, s3 - rate * x3
 
         before, after = project(0), project(1)
-        before, after = settle(before, lead_gain), settle(after, gain)
+        before, after = settle(before, lead_gain, sides_lead), settle(after, gain, sides_own)
 
         @pl.when(k > 1)
         def _():
@@ -476,7 +514,6 @@
             first([unpack(par[w]) for w in range(W)])
 
         d_lead, c_lead = nudge(before, [tx[i] for i in range(5)], lead_gain)
-        tables[9].wait()
         def widen(x):
             return jnp.concatenate([x, jnp.zeros_like(x)], 1)
 
@@ -487,9 +524,9 @@
             d1, d2, d3 = d
             e1 = split(d1)
             main = d3 + small[10] * d2 + small[11] * d1
-            rows = dot3(table(0), d2 + small[12] * d1) + dot3(table(1), e1)
+            rows = dotk(ends[0], d2 + small[12] * d1) + dotk(ends[1], e1)
             cols = dot3t(table(2), d2 + small[13] * d1) + dot3t(table(3), e1)
-            corner = dot3(dot3(table(0), e1), (up[0, 64:], up[1, 64:]))
+            corner = dot3(dotk(ends[0], e1), (up[0, 64:], up[1, 64:]))
             return jnp.concatenate([pack(main), (widen(rows + cols) + corner)[:8]], 0)
 
         def mend(i, g):
@@ -555,6 +592,7 @@
     tables[2].wait()
     tables[3].wait()
 
+    u_wide = tri((u_t[0], u_t[1]))
     most = L // 2
     far = jnp.where(2 * px < PX, 0, 1)
     for i in range(2):
@@ -563,7 +601,7 @@
         some = pl.ds(first, most)
         settled(fix.at[some], f_recv.at[turn])
         half = [dot3(unpack_fix(fix[first + j], m), (vt_t[0], vt_t[1])) for j in range(most)]
-        done = [calm[first + j] + dot3((u_t[0], u_t[1]), half[j]) for j in range(most)]
+        done = [calm[first + j] + dotk(u_wide, half[j]) for j in range(most)]
         for j in range(most):
             state[first + j] = done[j]
         pltpu.make_async_copy(state.at[some], out.at[some], out_sem).start()
@@ -646,10 +684,10 @@
          both, both**2, np.tile(2.0 * rate_y[None, :], (m, 1)), np.tile(2.0 * rate_x[:, None], (1, m)),
          both**3, np.tile(3.0 * rate_x[:, None] ** 2, (1, m))]
     ).astype(np.float32)
-    deep = (W + 1) * m
+    here = halves(np.swapaxes(u[:, :tall].reshape(PX, cx, tall), 1, 2))
     tables = [
         halves(u_few),
-        halves(np.swapaxes(u[:, :tall].reshape(PX, cx, tall), 1, 2)),
+        np.concatenate([here[0], here[0], here[1]], -1),
         halves(v),
         halves(v_few.T),
         halves(np.concatenate([t[m:tall].T for t in tu[1:]], 1)),
@@ -690,7 +728,7 @@
             pltpu.VMEM((8, 128), F32),
             pltpu.VMEM((8, 128), F32),
             pltpu.VMEM((5, m, m), F32),
-            pltpu.VMEM((2, tall, cx), BF16),
+            pltpu.VMEM((tall, 3 * cx), BF16),
             pltpu.VMEM((2, cy, lanes), BF16),
             pltpu.VMEM((2, m, 16 * W), BF16),
             pltpu.VMEM((2, 4 * m + 16 * W, m), BF16),

time: 19 us -> 18.9 us (level)
  no operation moved by 1% of the time
where the time goes in v7:
time: 18.9 us; the launch traced here: 18.8 us
  Pallas kernels  18.2 us (96%)
  between operations  0.64 us (3%)
    pallas_call x1, Pallas kernels, body(): pl.pallas_call(functools.partial(kernel, dims, owners), out_shape=(pltpu....  17.4 us
    pallas_call x1, Pallas kernels, body(): pl.pallas_call(store, out_shape=[jax.ShapeDtypeStruct((1, L, cx, cy), F32...  0.76 us

profile of v7, /device:TPU:3, one launch (start us, length us, event | category | flops | bytes accessed | tf_op | source)
XLA Modules:
  0.0 18.8 jit_solution(18013739140668094174)
XLA Ops:
  0.6 17.4 %shard_map.131 = (f32[4,64,128]{2,1,0:T(8,128)S(1)}, f32[4,32,128]{2,1,0:T(8,128)S(1)}) custom-call(f32[1,4,64,128]{3,2,1,0:T(8,128)} %field.1, f32[3,4,64,64]{3,2,1,0:T(8,128)} %drive.1, f32[1,4]{1,0:T(1,128)} %relax_hbm.1, s32[2,4]{1,0:T(2,128)} %bitcast.1, bf16[2,256,80]{2,1,0:T(8,128)(2,1)} %constant.16.clone.u_hbm, ...), custom_call_target="tpu_custom_call" | custom-call | tf_op jit(solution)/shard_map/pallas_call | solution.py:702
  18.0 0.8 %shard_map.132 = (f32[1,4,64,128]{3,2,1,0:T(8,128)}, f32[1,4,64,64]{3,2,1,0:T(8,128)}) custom-call(f32[4,64,128]{2,1,0:T(8,128)S(1)} %get-tuple-element.4.state, f32[4,32,128]{2,1,0:T(8,128)S(1)} %get-tuple-element.5.packed), custom_call_target="tpu_custom_call" | custom-call | tf_op jit(solution)/shard_map/pallas_call | solution.py:754

commit v8 on v7

--- a/solution.py
+++ b/solution.py
@@ -260,7 +260,7 @@
 
     def beam(src, dst, i, device):
         return pltpu.make_async_remote_copy(
-            src_ref=src, dst_ref=dst, send_sem=h_send.at[i], recv_sem=h_recv.at[i],
+            src_ref=src, dst_ref=dst, send_sem=h_send.at[i // 2], recv_sem=h_recv.at[i // 2],
             device_id=device, device_id_type=MESH,
         )
 
@@ -278,10 +278,17 @@
         def _():
             halo[i].start()
 
-    def land_halo(i):
-        @pl.when(sides[i ^ 1][0])
-        def _():
-            halo[i].wait_recv()
+    def settle_halo(i, sem):
+        lower, upper = sides[2 * i][0], sides[2 * i + 1][0]
+        two, one = (wide.at[:, pl.ds(0, 16)], wide.at[:, pl.ds(0, 8)]) if i == 0 else (near, near.at[0])
+
+        @pl.when(jnp.logical_and(lower, upper))
+        def _():
+            settled(two, sem)
+
+        @pl.when(lower != upper)
+        def _():
+            settled(one, sem)
 
     for l, o in enumerate(owners):
         @pl.when(jnp.logical_not(owns[l]))
@@ -334,8 +341,7 @@
     start_halo(3)
 
     def widen_patch():
-        land_halo(2)
-        land_halo(3)
+        settle_halo(1, h_recv.at[1])
         after, before = near[1], near[0]
         for l in range(L):
             for i in range(folds):
@@ -350,8 +356,7 @@
         start_halo(1)
 
     def run_free():
-        land_halo(0)
-        land_halo(1)
+        settle_halo(0, h_recv.at[0])
         shape = (cx + 16, cy + 128)
         row = lax.broadcasted_iota(jnp.int32, shape, 0) + (px * cx - 8)
         col = lax.broadcasted_iota(jnp.int32, shape, 1)
@@ -624,10 +629,8 @@
     def _():
         gain_out.wait_send()
 
-    for i in range(4):
-        @pl.when(sides[i][0])
-        def _():
-            halo[i].wait_send()
+    settle_halo(0, h_send.at[0])
+    settle_halo(1, h_send.at[1])
     settled(state, out_sem)
 
 
@@ -739,8 +742,8 @@
             dma((12,)),
             dma,
             dma,
-            dma((4,)),
-            dma((4,)),
+            dma((2,)),
+            dma((2,)),
             dma((2,)),
             dma((2,)),
             dma,

time: 18.9 us -> 18.9 us (level)
  no operation moved by 1% of the time
where the time goes in v8:
time: 18.9 us; the launch traced here: 18.8 us
  Pallas kernels  18.1 us (96%)
  between operations  0.64 us (3%)
    pallas_call x1, Pallas kernels, body(): pl.pallas_call(functools.partial(kernel, dims, owners), out_shape=(pltpu....  17.4 us
    pallas_call x1, Pallas kernels, body(): pl.pallas_call(store, out_shape=[jax.ShapeDtypeStruct((1, L, cx, cy), F32...  0.76 us

profile of v8, /device:TPU:3, one launch (start us, length us, event | category | flops | bytes accessed | tf_op | source)
XLA Modules:
  0.0 18.8 jit_solution(13101231489431780040)
XLA Ops:
  0.6 17.4 %shard_map.131 = (f32[4,64,128]{2,1,0:T(8,128)S(1)}, f32[4,32,128]{2,1,0:T(8,128)S(1)}) custom-call(f32[1,4,64,128]{3,2,1,0:T(8,128)} %field.1, f32[3,4,64,64]{3,2,1,0:T(8,128)} %drive.1, f32[1,4]{1,0:T(1,128)} %relax_hbm.1, s32[2,4]{1,0:T(2,128)} %bitcast.1, bf16[2,256,80]{2,1,0:T(8,128)(2,1)} %constant.16.clone.u_hbm, ...), custom_call_target="tpu_custom_call" | custom-call | tf_op jit(solution)/shard_map/pallas_call | solution.py:705
  18.0 0.8 %shard_map.132 = (f32[1,4,64,128]{3,2,1,0:T(8,128)}, f32[1,4,64,64]{3,2,1,0:T(8,128)}) custom-call(f32[4,64,128]{2,1,0:T(8,128)S(1)} %get-tuple-element.4.state, f32[4,32,128]{2,1,0:T(8,128)S(1)} %get-tuple-element.5.packed), custom_call_target="tpu_custom_call" | custom-call | tf_op jit(solution)/shard_map/pallas_call | solution.py:757

commit v9 on v8

--- a/solution.py
+++ b/solution.py
@@ -121,10 +121,10 @@
 def kernel(
     dims, owners,
     field, drive, relax_hbm, offs_hbm,
-    u_hbm, ut_hbm, v_hbm, vt_hbm, left_hbm, right_hbm, up_hbm, small_hbm,
+    u_hbm, ut_hbm, v_hbm, vt_hbm, up_hbm, small_hbm,
     out, modes,
     fvm, pbuf, abuf, strip, near, wide, calm, state, fix, tally, u_t, vt_t, zbuf, mail, start, par, cbuf, lead, glead, tx,
-    ut_t, v_t, left, right, up, small, relax, offs,
+    ut_t, v_t, up, small, relax, offs,
     load_sem, a_send, a_recv, h_send, h_recv, c_sem, g_sem, out_sem, b_send, f_recv, m_recv,
 ):
     nests, PY, PX, L, cx, cy, m, W = dims
@@ -172,7 +172,7 @@
         (v_hbm.at[:, cols_here], v_t), (ut_hbm.at[px], ut_t),
         (u_hbm.at[:, rows_here], u_t), (vt_hbm.at[:, :, cols_here], vt_t),
         (relax_hbm, relax), (offs_hbm, offs), (small_hbm, small),
-        (left_hbm, left), (right_hbm, right), (up_hbm, up),
+        (up_hbm, up),
     ]
     tables = [
         pltpu.make_async_copy(src, dst, load_sem.at[2 + i]) for i, (src, dst) in enumerate(pairs)
@@ -453,10 +453,8 @@
             first([start[w] for w in range(W)])
 
         tables[7].wait()
-        tables[8].wait()
-
-        grown = [tri((left[0, :, : 16 * i], left[1, :, : 16 * i])) for i in (1, 2, 3)]
-        tables[9].wait()
+
+        grown = [tri((up[0, 64 + m : 64 + 2 * m, : 16 * i], up[1, 64 + m : 64 + 2 * m, : 16 * i])) for i in (1, 2, 3)]
         ends = [tri((up[0, 16 * i : 16 * i + 16, :m], up[1, 16 * i : 16 * i + 16, :m])) for i in (0, 1)]
         settled(abuf.at[pl.ds(0, 2 * G - 1)], a_recv)
 
@@ -470,7 +468,8 @@
             return total
 
         def table(start, size):
-            return right[0, start : start + size], right[1, start : start + size]
+            start += 64 + 2 * m
+            return up[0, start : start + size, :m], up[1, start : start + size, :m]
 
         def rows(*parts):
             return dotk(grown[len(parts) - 1], jnp.concatenate(parts, 0))
@@ -531,7 +530,7 @@
             main = d3 + small[10] * d2 + small[11] * d1
             rows = dotk(ends[0], d2 + small[12] * d1) + dotk(ends[1], e1)
             cols = dot3t(table(2), d2 + small[13] * d1) + dot3t(table(3), e1)
-            corner = dot3(dotk(ends[0], e1), (up[0, 64:], up[1, 64:]))
+            corner = dot3(dotk(ends[0], e1), (up[0, 64 : 64 + m], up[1, 64 : 64 + m]))
             return jnp.concatenate([pack(main), (widen(rows + cols) + corner)[:8]], 0)
 
         def mend(i, g):
@@ -546,7 +545,7 @@
 
         def give(copy, i):
             def one(j):
-                g = jnp.where(2 * px < PX, G - 1 - j, j)
+                g = j
                 if i == 0:
                     copy(i, g).start()
                 else:
@@ -693,9 +692,12 @@
         np.concatenate([here[0], here[0], here[1]], -1),
         halves(v),
         halves(v_few.T),
-        halves(np.concatenate([t[m:tall].T for t in tu[1:]], 1)),
-        halves(np.concatenate(tv[1:3] + [t[m : m + 16] for t in tv[1:]], 0)),
-        halves(np.concatenate([np.pad(ends.reshape(64, m), ((0, 0), (0, m))), corner], 0)),
+        halves(np.concatenate([
+            np.pad(ends.reshape(64, m), ((0, 0), (0, m))),
+            corner,
+            np.pad(np.concatenate([t[m:tall].T for t in tu[1:]], 1), ((0, 0), (0, lanes - 16 * W))),
+            np.pad(np.concatenate(tv[1:3] + [t[m : m + 16] for t in tv[1:]], 0), ((0, 0), (0, m))),
+        ], 0)),
     ]
     any_space = pl.BlockSpec(memory_space=pl.ANY)
     vmem = pl.BlockSpec(memory_space=pltpu.VMEM)
@@ -708,7 +710,7 @@
             pltpu.VMEM((L, cx, cy), F32),
             pltpu.VMEM((L, m // 2, lanes), F32),
         ),
-        in_specs=[any_space] * 12,
+        in_specs=[any_space] * 10,
         out_specs=(any_space, any_space),
         scratch_shapes=[
             pltpu.VMEM((L, cx, cy), F32),
@@ -733,13 +735,11 @@
             pltpu.VMEM((5, m, m), F32),
             pltpu.VMEM((tall, 3 * cx), BF16),
             pltpu.VMEM((2, cy, lanes), BF16),
-            pltpu.VMEM((2, m, 16 * W), BF16),
-            pltpu.VMEM((2, 4 * m + 16 * W, m), BF16),
-            pltpu.VMEM((2, 64 + m, lanes), BF16),
+            pltpu.VMEM((2, 64 + 6 * m + 16 * W, lanes), BF16),
             pltpu.VMEM((16, m, m), F32),
             pltpu.SMEM(relax_rates.shape, F32),
             pltpu.SMEM(nest_offsets.shape[::-1], jnp.int32),
-            dma((12,)),
+            dma((10,)),
             dma,
             dma,
             dma((2,)),

time: 18.9 us -> 18.9 us (level)
  no operation moved by 1% of the time
where the time goes in v9:
time: 18.9 us; the launch traced here: 18.7 us
  Pallas kernels  18.1 us (96%)
  between operations  0.64 us (3%)
    pallas_call x1, Pallas kernels, body(): pl.pallas_call(functools.partial(kernel, dims, owners), out_shape=(pltpu....  17.3 us
    pallas_call x1, Pallas kernels, body(): pl.pallas_call(store, out_shape=[jax.ShapeDtypeStruct((1, L, cx, cy), F32...  0.76 us

profile of v9, /device:TPU:3, one launch (start us, length us, event | category | flops | bytes accessed | tf_op | source)
XLA Modules:
  0.0 18.7 jit_solution(16029083670427247177)
XLA Ops:
  0.6 17.3 %shard_map.113 = (f32[4,64,128]{2,1,0:T(8,128)S(1)}, f32[4,32,128]{2,1,0:T(8,128)S(1)}) custom-call(f32[1,4,64,128]{3,2,1,0:T(8,128)} %field.1, f32[3,4,64,64]{3,2,1,0:T(8,128)} %drive.1, f32[1,4]{1,0:T(1,128)} %relax_hbm.1, s32[2,4]{1,0:T(2,128)} %bitcast.1, bf16[2,256,80]{2,1,0:T(8,128)(2,1)} %constant.12.clone.u_hbm, ...), custom_call_target="tpu_custom_call" | custom-call | tf_op jit(solution)/shard_map/pallas_call | solution.py:707
  18.0 0.8 %shard_map.114 = (f32[1,4,64,128]{3,2,1,0:T(8,128)}, f32[1,4,64,64]{3,2,1,0:T(8,128)}) custom-call(f32[4,64,128]{2,1,0:T(8,128)S(1)} %get-tuple-element.4.state, f32[4,32,128]{2,1,0:T(8,128)S(1)} %get-tuple-element.5.packed), custom_call_target="tpu_custom_call" | custom-call | tf_op jit(solution)/shard_map/pallas_call | solution.py:757
